TPU v7x, 32 devices: a whole 2x2x4 slice. The times are simulated.
32 devices in a mesh: parts: 2 (over x), seq: 16 (over z, y, core).
Axes of the slice: x: 2, y: 2, z: 4, core: 2. Of those that a mesh axis runs over, the one named last changes fastest.
Arguments:
- queries: bfloat16 [3072, 1024], P(('parts', 'seq')), parts along dimension 0, may hold values from -8 to 8
- self_keys: bfloat16 [3072, 1024], P(('parts', 'seq')), parts along dimension 0, may hold values from -8 to 8
- self_values: bfloat16 [3072, 1024], P(('parts', 'seq')), parts along dimension 0, may hold values from -8 to 8
- residual_in: bfloat16 [3072, 1024], P(('parts', 'seq')), parts along dimension 0, may hold values from -0.23925781 to 0.23925781
- text_keys: bfloat16 [2, 8, 256, 1024], P(None, 'parts', None, 'seq'), parts along dimension 1, may hold values from -8 to 8
- text_values: bfloat16 [2, 8, 256, 1024], P(None, 'parts', None, 'seq'), parts along dimension 1, may hold values from -8 to 8
- text_lengths: int32 [2, 8], P(None, 'parts'), parts along dimension 1, may hold values from 2 to 256
- frame_counts: int32 [8], P('parts'), parts along dimension 0, may hold values from 1 to 16, 24 in all
- mod_gain: float32 [1024], replicated, may hold values from 0.1 to 1.9
- mod_shift: float32 [1024], replicated, may hold values from -1.8 to 1.8
- head_weight: bfloat16 [1024, 64], replicated, may hold values from -0.1875 to 0.1875
- head_bias: float32 [64], replicated, may hold values from -1.8 to 1.8
- guide_scale: float32 [1], replicated, may hold values from 3 to 7
Outputs:
- guided: float32 [1536, 64], P(('parts', 'seq')), parts along dimension 0
There are 2 independent parts, one for each index of `parts`. A program takes and returns all parts, laid end to end along the dimension named above; an argument that names none is the same for every part. Nothing has to cross between parts.
Inputs may be any that keep to these rules, and one draw needn't show every extreme that they name: `frame_counts`: latent frames of the 4 videos in packing order; they sum to 24 and the largest is exactly 16. `text_lengths`: live prompt tokens, counted from the front of each prompt.
All inputs are finite; a program needn't handle non-finite values.
Results may differ from a plain program's by a relative error of at most 0.0049.
Values may be sent and summed in bfloat16 or wider, within the bound.
No kernel may reach another device: no remote copies, remote signals or barrier semaphores. Data moves between devices by JAX's collectives and lax.ppermute only.
A program may use at most 64 MiB of HBM per device.

v0:
```python
import functools
import math

import jax
import jax.numpy as jnp
from jax import lax
from jax.experimental import pallas as pl
from jax.experimental.pallas import tpu as pltpu
from jax.sharding import PartitionSpec as P

HEAD_CHANNELS = 128
TPF = 32
SCALE = HEAD_CHANNELS ** (-0.5)
LOG2E = math.log2(math.e)
UNROLL_CHIPS = 8
STRIP = 8
LATE = 3


def params(mib):
    return pltpu.CompilerParams(vmem_limit_bytes=mib << 20)


VMEM = pl.BlockSpec(memory_space=pltpu.VMEM)
SMEM = pl.BlockSpec(memory_space=pltpu.SMEM)
HBM = pl.BlockSpec(memory_space=pltpu.HBM)


def chip_pairs(devices, index):
    return [(d, d ^ (2 * hop(index, devices // 2, d % 2))) for d in range(devices)]


def core_pairs(devices):
    return [(source, source ^ 1) for source in range(devices)]


def hop(index, chips, core):
    return (1 - core) * (index // 2 + (index % 2) * (chips // 2)) + core * (index)


def my_chip():
    return lax.axis_index("seq") // 2


def my_core():
    return lax.axis_index("seq") % 2


def rows(start, size):
    if isinstance(start, int):
        return pl.ds(start, size)
    return pl.ds(pl.multiple_of(start, TPF), size)


def pack_kernel(chips, *refs):
    sources, small, residual = refs[:3], refs[3:6], refs[6]
    blocks, kept, (own, other, sems) = refs[7 : 7 + chips], refs[7 + chips : 10 + chips], refs[10 + chips :]
    tok = sources[0].shape[0]
    chip, core = my_chip(), my_core()
    copies = []
    for index in range(chips):
        head = chip ^ hop(index, chips, core)
        cols = pl.ds(pl.multiple_of(head * HEAD_CHANNELS, HEAD_CHANNELS), HEAD_CHANNELS)
        for part, source in enumerate(sources):
            target = blocks[index].at[pl.ds(part * tok, tok)]
            copies.append(pltpu.make_async_copy(source.at[:, cols], target, sems.at[len(copies)]))
    half = tok // 2
    halves = [residual.at[pl.ds(pl.multiple_of(c * half, 16), half)] for c in (core, 1 - core)]
    for source, target in zip(list(small) + halves, list(kept) + [own, other]):
        copies.append(pltpu.make_async_copy(source, target, sems.at[len(copies)]))
    for copy in copies:
        copy.start()
    for copy in copies:
        copy.wait()


def softmax(scores):
    top = jnp.max(scores, axis=-1, keepdims=True)
    raised = jnp.exp2((scores - top) * (SCALE * LOG2E))
    share = 1.0 / jnp.sum(raised, axis=-1, keepdims=True)
    return (raised * share).astype(jnp.bfloat16)


def repeat(count, body):
    if count <= UNROLL_CHIPS:
        for index in range(count):
            body(index, 0)
    else:
        lax.fori_loop(0, count, body, 0)


def dot_last(a, b):
    return lax.dot_general(a, b, (((1,), (1,)), ((), ())), preferred_element_type=jnp.float32)


def video_ends(counts_ref):
    ends, end = [], jnp.int32(0)
    for video in range(counts_ref.shape[0]):
        end = end + counts_ref[video] * TPF
        ends.append(end)
    return ends


def video_of(place, ends):
    return sum((place >= e).astype(jnp.int32) for e in ends[:-1])


def prompt(queries, keys, values, length):
    scores = jnp.dot(queries, keys, preferred_element_type=jnp.float32)
    place = lax.broadcasted_iota(jnp.int32, (1, keys.shape[1]), 1)
    return dot_last(softmax(jnp.where(place < length, scores, -1e30)), values)


def early_kernel(chips, counts_ref, lengths_ref, tk_own, tv_own, tk_other, tv_other, *rest):
    blocks = rest[:-4]
    cross, tk, tv, qs = rest[-4:]
    early, tok = cross.shape[:2]
    videos, half = tk_own.shape[1:3]
    chip, core = my_chip(), my_core()
    ends = video_ends(counts_ref)
    own_rows = pl.ds(pl.multiple_of(core * half, half), half)
    other_rows = pl.ds(pl.multiple_of((1 - core) * half, half), half)
    for video in range(videos):
        tk[video, own_rows, :] = tk_own[core, video]
        tk[video, other_rows, :] = tk_other[core, video]
        tv[video, own_rows, :] = tv_own[core, video]
        tv[video, other_rows, :] = tv_other[core, video]
    for index in range(early):
        qs[index] = blocks[index][pl.ds(0, tok), :]

    def one(index, carry):
        video = video_of((chip ^ hop(index, chips, core)) * tok, ends)
        cross[index] = prompt(qs[index], tk[video], tv[video], lengths_ref[core, video])
        return carry

    repeat(early, one)


def attend_kernel(chips, counts_ref, lengths_ref, tk, tv, early_ref, *rest):
    blocks, out_ref = rest[:chips], rest[chips]
    qs, ks, vs, cross, raw, weights = rest[chips + 1 :]
    tok = cross.shape[1]
    total = chips * tok
    strip = raw.shape[0]
    chip, core = my_chip(), my_core()
    ends = video_ends(counts_ref)
    for index in range(chips):
        h = chip ^ hop(index, chips, core)
        at = rows(h * tok, tok)
        for part, target in enumerate((qs, ks, vs)):
            target[at, :] = blocks[index][pl.ds(part * tok, tok), :]

    def prompt_of(h, video):
        queries = qs[rows(h * tok, tok), :]
        return prompt(queries, tk[video], tv[video], lengths_ref[core, video])

    for index in range(chips):
        h = chip ^ hop(index, chips, core)
        if index < early_ref.shape[0]:
            cross[h] = early_ref[index]
        else:
            cross[h] = prompt_of(h, video_of(h * tok, ends))
    for video in range(1, len(ends)):
        h = ends[video - 1] // tok
        row_video = video_of(h * tok + lax.broadcasted_iota(jnp.int32, (tok, 1), 0), ends)
        cross[h] = jnp.where(row_video == video, prompt_of(h, video), cross[h])

    key_video = video_of(lax.broadcasted_iota(jnp.int32, (1, total), 1), ends)

    def one_strip(index, carry):
        base = index * strip
        raw[...] = dot_last(qs[rows(base, strip), :], ks[...])
        for b in range(strip // tok):
            at = pl.ds(b * tok, tok)
            place = base + b * tok + lax.broadcasted_iota(jnp.int32, (tok, 1), 0)
            allowed = video_of(place, ends) == key_video
            weights[at, :] = softmax(jnp.where(allowed, raw[at, :], -1e30))
        out = jnp.dot(weights[...], vs[...], preferred_element_type=jnp.float32)
        for b in range(strip // tok):
            h = index * (strip // tok) + b
            out_ref[h] = (out[b * tok : (b + 1) * tok] + cross[h]).astype(jnp.bfloat16)
        return carry

    repeat(total // strip, one_strip)


def head_kernel(chips, scale_ref, x_ref, x_other, gain_ref, shift_ref, weight_ref, bias_ref, blocks, out_ref):
    _, width = x_ref.shape
    core = my_core()
    gain, shift = (ref[...].reshape(1, width) for ref in (gain_ref, shift_ref))

    def velocity(x, branch):
        attention = jnp.concatenate([blocks[2 * h + branch] for h in range(chips)], axis=-1)
        hidden = x.astype(jnp.float32) + attention.astype(jnp.float32)
        mean = jnp.sum(hidden, axis=-1, keepdims=True) * (1.0 / width)
        centred = hidden - mean
        var = jnp.sum(centred * centred, axis=-1, keepdims=True) * (1.0 / width)
        normed = centred * lax.rsqrt(var + 1e-06) * gain + shift
        return dot_last(normed.astype(jnp.bfloat16), weight_ref[...]) + bias_ref[...].reshape(1, -1)

    own, other = velocity(x_ref[...], core), velocity(x_other[...], 1 - core)
    scale = scale_ref[0]
    share = jnp.where(core == 0, scale, 1.0 - scale)
    out_ref[...] = other + share * (own - other)


def local(
    queries,
    self_keys,
    self_values,
    residual_in,
    text_keys,
    text_values,
    text_lengths,
    frame_counts,
    mod_gain,
    mod_shift,
    head_weight,
    head_bias,
    guide_scale,
):
    devices = lax.axis_size("seq")
    chips = devices // 2
    tok, width = queries.shape
    total = chips * tok
    bf16, f32 = jnp.bfloat16, jnp.float32
    block_shape = jax.ShapeDtypeStruct((3 * tok, HEAD_CHANNELS), bf16)
    text_keys = jnp.swapaxes(text_keys, 2, 3)
    text_values = jnp.swapaxes(text_values, 2, 3)
    vectors = (mod_gain, mod_shift, head_bias)
    packed = pl.pallas_call(
        functools.partial(pack_kernel, chips),
        out_shape=[block_shape] * chips + [jax.ShapeDtypeStruct(v.shape, v.dtype) for v in vectors]
        + [jax.ShapeDtypeStruct((tok // 2, width), bf16)] * 2,
        in_specs=[HBM] * 7,
        out_specs=[VMEM] * (chips + 5),
        scratch_shapes=[pltpu.SemaphoreType.DMA((3 * chips + 5,))],
        compiler_params=params(8),
        name="pack",
    )(*(pltpu.with_memory_space_constraint(x, pltpu.HBM) for x in (queries, self_keys, self_values) + vectors + (residual_in,)))
    blocks, vectors, (x_own, x_other) = list(packed[:chips]), packed[chips:-2], packed[-2:]
    for index in range(1, chips):
        blocks[index] = lax.ppermute(blocks[index], "seq", chip_pairs(devices, index))
    other_keys = lax.ppermute(text_keys, "seq", core_pairs(devices))
    other_values = lax.ppermute(text_values, "seq", core_pairs(devices))
    x_other = lax.ppermute(x_other, "seq", core_pairs(devices))

    videos, half, text = text_keys.shape[1:]
    tokens = pltpu.VMEM((total, HEAD_CHANNELS), bf16)
    strip = math.gcd(chips, STRIP) * tok
    early = max(chips - LATE, 1)
    prompts = jax.ShapeDtypeStruct((videos, 2 * half, text), bf16)
    cross, keys, values = pl.pallas_call(
        functools.partial(early_kernel, chips),
        out_shape=[
            jax.ShapeDtypeStruct((early, tok, HEAD_CHANNELS), f32),
            prompts,
            prompts,
        ],
        in_specs=[SMEM] * 2 + [VMEM] * (4 + early),
        out_specs=[VMEM] * 3,
        scratch_shapes=[pltpu.VMEM((early, tok, HEAD_CHANNELS), bf16)],
        cost_estimate=pl.CostEstimate(
            flops=4 * early * tok * text * HEAD_CHANNELS,
            bytes_accessed=4 * total * HEAD_CHANNELS,
            transcendentals=early * tok * text,
        ),
        compiler_params=params(12),
        name="early",
    )(frame_counts, text_lengths, text_keys, text_values, other_keys, other_values, *blocks[:early])
    attended = pl.pallas_call(
        functools.partial(attend_kernel, chips),
        out_shape=jax.ShapeDtypeStruct((chips, tok, HEAD_CHANNELS), bf16),
        in_specs=[SMEM] * 2 + [VMEM] * (3 + chips),
        out_specs=VMEM,
        scratch_shapes=[tokens] * 3
        + [
            pltpu.VMEM((chips, tok, HEAD_CHANNELS), f32),
            pltpu.VMEM((strip, total), f32),
            pltpu.VMEM((strip, total), bf16),
        ],
        cost_estimate=pl.CostEstimate(
            flops=4 * total * total * HEAD_CHANNELS,
            bytes_accessed=8 * total * HEAD_CHANNELS,
            transcendentals=total * total,
        ),
        compiler_params=params(24),
        name="attend",
    )(frame_counts, text_lengths, keys, values, cross, *blocks)
    returned = lax.all_to_all(
        attended.reshape(devices, tok // 2, HEAD_CHANNELS), "seq", split_axis=0, concat_axis=0, tiled=True
    )

    return pl.pallas_call(
        functools.partial(head_kernel, chips),
        out_shape=jax.ShapeDtypeStruct((tok // 2, head_weight.shape[1]), f32),
        in_specs=[SMEM] + [VMEM] * 7,
        out_specs=VMEM,
        compiler_params=params(8),
        name="head",
    )(guide_scale, x_own, x_other, vectors[0], vectors[1], head_weight.T, vectors[2], returned)


def solution(mesh):
    return jax.shard_map(
        local,
        mesh=mesh,
        in_specs=(
            P(("parts", "seq"), None),
            P(("parts", "seq"), None),
            P(("parts", "seq"), None),
            P(("parts", "seq"), None),
            P(None, "parts", None, "seq"),
            P(None, "parts", None, "seq"),
            P(None, "parts"),
            P("parts"),
            P(),
            P(),
            P(),
            P(),
            P(),
        ),
        out_specs=P(("parts", "seq"), None),
        check_vma=False,
    )
```

profile of v0, /device:TPU:0, one launch (start us, length us, event | category | flops | bytes accessed | tf_op | source)
XLA Modules:
  0.0 43.4 jit_solution(12614045480677894088)
XLA Ops:
  0.0 0.5 %collective-permute-start.1 = (bf16[2,4,64,256]{3,2,1,0:T(8,128)(2,1)}, bf16[2,4,64,256]{3,2,1,0:T(8,128)(2,1)S(1)}, u32[]{:S(2)}, u32[]{:S(2)}) collective-permute-start(bf16[2,4,64,256]{3,2,1,0:T(8,128)(2,1)} %bitcast.4), channel_id=1, source_target_pairs={{0,1},{1,0},{2,3},{3,2},{4,5},{5,4},{6,7},{7,6},{8,9},{9,8},{10,11... | collective-permute-start | bytes 786440 | tf_op jit(solution)/shard_map/ppermute | solution.py:244
  0.5 0.0 copy-start
  0.5 0.0 copy-start.1
  0.5 0.1 collective-permute-start.2
  0.6 1.5 %pack.1 = (bf16[288,128]{1,0:T(8,128)(2,1)S(1)}, bf16[288,128]{1,0:T(8,128)(2,1)S(1)}, bf16[288,128]{1,0:T(8,128)(2,1)S(1)}, bf16[288,128]{1,0:T(8,128)(2,1)S(1)...) custom-call(bf16[96,1024]{1,0:T(8,128)(2,1)} %refs_0_.1, ...), custom_call_target="tpu_custom_call" | custom-call | tf_op jit(solution)/shard_map/pack/pallas_call | solution.py:231
  2.1 4.0 %collective-permute-start.3 = (bf16[288,128]{1,0:T(8,128)(2,1)S(1)}, bf16[288,128]{1,0:T(8,128)(2,1)S(1)}, u32[]{:S(2)}, u32[]{:S(2)}) collective-permute-start(bf16[288,128]{1,0:T(8,128)(2,1)S(1)} %get-tuple-element.27), channel_id=1, source_target_pairs={{0,8},{1,3},{2,10},{3,1},{4,12},{5,7},{6,14},{7,5},{8,0},{9,11},{1... | collective-permute-start | bytes 221192 | tf_op jit(solution)/shard_map/ppermute | solution.py:243
  6.1 1.5 %collective-permute-start.4 = (bf16[288,128]{1,0:T(8,128)(2,1)S(1)}, bf16[288,128]{1,0:T(8,128)(2,1)S(1)}, u32[]{:S(2)}, u32[]{:S(2)}) collective-permute-start(bf16[288,128]{1,0:T(8,128)(2,1)S(1)} %get-tuple-element.28), channel_id=1, source_target_pairs={{0,2},{1,5},{2,0},{3,7},{4,6},{5,1},{6,4},{7,3},{8,10},{9,13},{10,... | collective-permute-start | bytes 221192 | tf_op jit(solution)/shard_map/ppermute | solution.py:243
  7.6 0.0 collective-permute-start.5
  7.7 1.1 %collective-permute-done.3.rest_1_ = bf16[288,128]{1,0:T(8,128)(2,1)S(1)} collective-permute-done((bf16[288,128]{1,0:T(8,128)(2,1)S(1)}, bf16[288,128]{1,0:T(8,128)(2,1)S(1)}, u32[]{:S(2)}, u32[]{:S(2)}) %collective-permute-start.3) | collective-permute-done | bytes 73760 | tf_op jit(solution)/shard_map/ppermute | solution.py:243
  8.8 1.9 %collective-permute-start.6 = (bf16[288,128]{1,0:T(8,128)(2,1)S(1)}, bf16[288,128]{1,0:T(8,128)(2,1)S(1)}, u32[]{:S(2)}, u32[]{:S(2)}) collective-permute-start(bf16[288,128]{1,0:T(8,128)(2,1)S(1)} %get-tuple-element.30), channel_id=1, source_target_pairs={{0,4},{1,9},{2,6},{3,11},{4,0},{5,13},{6,2},{7,15},{8,12},{9,1},{1... | collective-permute-start | bytes 221192 | tf_op jit(solution)/shard_map/ppermute | solution.py:243
  10.7 0.6 %collective-permute-done.4.rest_2_ = bf16[288,128]{1,0:T(8,128)(2,1)S(1)} collective-permute-done((bf16[288,128]{1,0:T(8,128)(2,1)S(1)}, bf16[288,128]{1,0:T(8,128)(2,1)S(1)}, u32[]{:S(2)}, u32[]{:S(2)}) %collective-permute-start.4) | collective-permute-done | bytes 73760 | tf_op jit(solution)/shard_map/ppermute | solution.py:243
  11.3 2.4 %collective-permute-start.7 = (bf16[288,128]{1,0:T(8,128)(2,1)S(1)}, bf16[288,128]{1,0:T(8,128)(2,1)S(1)}, u32[]{:S(2)}, u32[]{:S(2)}) collective-permute-start(bf16[288,128]{1,0:T(8,128)(2,1)S(1)} %get-tuple-element.34), channel_id=1, source_target_pairs={{0,12},{1,11},{2,14},{3,9},{4,8},{5,15},{6,10},{7,13},{8,4},{9,3},... | collective-permute-start | bytes 221192 | tf_op jit(solution)/shard_map/ppermute | solution.py:243
  13.6 2.5 %collective-permute-done.5.rest_3_ = bf16[288,128]{1,0:T(8,128)(2,1)S(1)} collective-permute-done((bf16[288,128]{1,0:T(8,128)(2,1)S(1)}, bf16[288,128]{1,0:T(8,128)(2,1)S(1)}, u32[]{:S(2)}, u32[]{:S(2)}) %collective-permute-start.5) | collective-permute-done | bytes 73760 | tf_op jit(solution)/shard_map/ppermute | solution.py:243
  16.2 0.0 collective-permute-start.8
  16.2 0.0 collective-permute-done.6.rest_4_
  16.2 0.0 copy-start.3
  16.2 0.0 copy-start.4
  16.2 5.1 %collective-permute-start.9 = (bf16[288,128]{1,0:T(8,128)(2,1)S(1)}, bf16[288,128]{1,0:T(8,128)(2,1)S(1)}, u32[]{:S(2)}, u32[]{:S(2)}) collective-permute-start(bf16[288,128]{1,0:T(8,128)(2,1)S(1)} %get-tuple-element.36), channel_id=1, source_target_pairs={{0,14},{1,15},{2,12},{3,13},{4,10},{5,11},{6,8},{7,9},{8,6},{9,7},... | collective-permute-start | bytes 221192 | tf_op jit(solution)/shard_map/ppermute | solution.py:243
  21.3 0.0 collective-permute-done.1.tk_other
  21.3 0.0 collective-permute-done.2.tv_other
  21.3 0.0 copy-done
  21.3 0.0 copy-done.1
  21.3 0.0 copy-done.3
  21.3 0.0 copy-done.4
  21.3 1.4 %early.1 = (f32[5,96,128]{2,1,0:T(8,128)S(1)}, bf16[4,128,256]{2,1,0:T(8,128)(2,1)S(1)}, bf16[4,128,256]{2,1,0:T(8,128)(2,1)S(1)}) custom-call(s32[4]{0:T(128)S(1)} %copy-done.4, s32[2,4]{1,0:T(2,128)S(1)} %copy-done.3, bf16[2,4,64,256]{3,2,1,0:T(8,128)(2,1)S(1)} %bitcast.5, bf16[2,4,64,256]{3,2,1,0:T(8,128)(2,1)S(1)} %bitcast.7, ...), custom_call_target="tpu_custom_call" | custom-call | flops 62914560 | bytes 393216 | tf_op jit(solution)/shard_map/early/pallas_call | solution.py:253
  22.8 0.0 collective-permute-done.7.rest_5_
  22.8 0.0 collective-permute-done.8.rest_6_
  22.8 0.8 %collective-permute-done.9.rest_7_ = bf16[288,128]{1,0:T(8,128)(2,1)S(1)} collective-permute-done((bf16[288,128]{1,0:T(8,128)(2,1)S(1)}, bf16[288,128]{1,0:T(8,128)(2,1)S(1)}, u32[]{:S(2)}, u32[]{:S(2)}) %collective-permute-start.9) | collective-permute-done | bytes 73760 | tf_op jit(solution)/shard_map/ppermute | solution.py:243
  23.6 3.5 %attend.1 = bf16[8,96,128]{2,1,0:T(8,128)(2,1)} custom-call(s32[4]{0:T(128)S(1)} %copy-done.4, s32[2,4]{1,0:T(2,128)S(1)} %copy-done.3, bf16[4,128,256]{2,1,0:T(8,128)(2,1)S(1)} %get-tuple-element.31.tk, bf16[4,128,256]{2,1,0:T(8,128)(2,1)S(1)} %get-tuple-element.32.tv, f32[5,96,128]{2,1,0:T(8,128)S(1)} %get-tuple-element.33.early_ref, ...), custom_call_target="tpu_custom_call" | custom-call | flops 301989888 | bytes 786432 | tf_op jit(solution)/shard_map/attend/pallas_call | solution.py:271
  27.2 0.0 copy-start.2
  27.2 6.2 %all-to-all-start = ((bf16[16,48,128]{2,1,0:T(8,128)(2,1)}), bf16[16,48,128]{2,1,0:T(8,128)(2,1)S(1)}, u32[]{:S(2)}, u32[]{:S(2)}) async-start(bf16[16,48,128]{2,1,0:T(8,128)(2,1)} %bitcast.3), calls=%async_computation | async-start | bytes 393216 | tf_op jit(solution)/shard_map/all_to_all | solution.py:290
  33.4 0.4 collective-permute-start
  34.5 0.4 collective-permute-done.x_other
  34.9 7.5 %all-to-all-done.blocks = bf16[16,48,128]{2,1,0:T(8,128)(2,1)S(1)} async-done(((bf16[16,48,128]{2,1,0:T(8,128)(2,1)}), bf16[16,48,128]{2,1,0:T(8,128)(2,1)S(1)}, u32[]{:S(2)}, u32[]{:S(2)}) %all-to-all-start) | async-done | bytes 196640 | tf_op jit(solution)/shard_map/all_to_all | solution.py:290
  42.4 0.0 copy-done.2
  42.4 1.0 %head.1 = f32[48,64]{1,0:T(8,128)} custom-call(f32[1]{0:T(128)S(6)} %copy.14.scale_ref, bf16[48,1024]{1,0:T(8,128)(2,1)S(1)} %get-tuple-element.21.x_ref, bf16[48,1024]{1,0:T(8,128)(2,1)S(1)} %collective-permute-done.x_other, f32[1024]{0:T(1024)S(1)} %get-tuple-element.23.gain_ref, f32[1024]{0:T(1024)S(1)} %get-tuple-element.24.shift_ref, ...), custom_call_target="tpu_custom_call" | custom-call | tf_op jit(solution)/shard_map/head/pallas_call | solution.py:294
Async XLA Ops:
  0.0 21.3 %collective-permute-start.1 = (bf16[2,4,64,256]{3,2,1,0:T(8,128)(2,1)}, bf16[2,4,64,256]{3,2,1,0:T(8,128)(2,1)S(1)}, u32[]{:S(2)}, u32[]{:S(2)}) collective-permute-start(bf16[2,4,64,256]{3,2,1,0:T(8,128)(2,1)} %bitcast.4), channel_id=1, source_target_pairs={{0,1},{1,0},{2,3},{3,2},{4,5},{5,4},{6,7},{7,6},{8,9},{9,8},{10,11... | collective-permute-start | bytes 786440 | tf_op jit(solution)/shard_map/ppermute | solution.py:244
  0.5 20.8 %copy-start = (bf16[2,4,256,64]{2,3,1,0:T(8,128)(2,1)S(1)}, bf16[2,4,256,64]{2,3,1,0:T(8,128)(2,1)}, u32[]{:S(2)}) copy-start(bf16[2,4,256,64]{2,3,1,0:T(8,128)(2,1)} %param.17) | copy-start | bytes 786436
  0.5 20.8 %copy-start.1 = (bf16[2,4,256,64]{2,3,1,0:T(8,128)(2,1)S(1)}, bf16[2,4,256,64]{2,3,1,0:T(8,128)(2,1)}, u32[]{:S(2)}) copy-start(bf16[2,4,256,64]{2,3,1,0:T(8,128)(2,1)} %param.18) | copy-start | bytes 786436
  0.5 20.8 %collective-permute-start.2 = (bf16[2,4,64,256]{3,2,1,0:T(8,128)(2,1)}, bf16[2,4,64,256]{3,2,1,0:T(8,128)(2,1)S(1)}, u32[]{:S(2)}, u32[]{:S(2)}) collective-permute-start(bf16[2,4,64,256]{3,2,1,0:T(8,128)(2,1)} %bitcast.6), channel_id=1, source_target_pairs={{0,1},{1,0},{2,3},{3,2},{4,5},{5,4},{6,7},{7,6},{8,9},{9,8},{10,11... | collective-permute-start | bytes 786440 | tf_op jit(solution)/shard_map/ppermute | solution.py:245
  2.1 6.7 %collective-permute-start.3 = (bf16[288,128]{1,0:T(8,128)(2,1)S(1)}, bf16[288,128]{1,0:T(8,128)(2,1)S(1)}, u32[]{:S(2)}, u32[]{:S(2)}) collective-permute-start(bf16[288,128]{1,0:T(8,128)(2,1)S(1)} %get-tuple-element.27), channel_id=1, source_target_pairs={{0,8},{1,3},{2,10},{3,1},{4,12},{5,7},{6,14},{7,5},{8,0},{9,11},{1... | collective-permute-start | bytes 221192 | tf_op jit(solution)/shard_map/ppermute | solution.py:243
  6.1 5.1 %collective-permute-start.4 = (bf16[288,128]{1,0:T(8,128)(2,1)S(1)}, bf16[288,128]{1,0:T(8,128)(2,1)S(1)}, u32[]{:S(2)}, u32[]{:S(2)}) collective-permute-start(bf16[288,128]{1,0:T(8,128)(2,1)S(1)} %get-tuple-element.28), channel_id=1, source_target_pairs={{0,2},{1,5},{2,0},{3,7},{4,6},{5,1},{6,4},{7,3},{8,10},{9,13},{10,... | collective-permute-start | bytes 221192 | tf_op jit(solution)/shard_map/ppermute | solution.py:243
  7.6 8.5 %collective-permute-start.5 = (bf16[288,128]{1,0:T(8,128)(2,1)S(1)}, bf16[288,128]{1,0:T(8,128)(2,1)S(1)}, u32[]{:S(2)}, u32[]{:S(2)}) collective-permute-start(bf16[288,128]{1,0:T(8,128)(2,1)S(1)} %get-tuple-element.29), channel_id=1, source_target_pairs={{0,10},{1,7},{2,8},{3,5},{4,14},{5,3},{6,12},{7,1},{8,2},{9,15},{1... | collective-permute-start | bytes 221192 | tf_op jit(solution)/shard_map/ppermute | solution.py:243
  8.8 7.4 %collective-permute-start.6 = (bf16[288,128]{1,0:T(8,128)(2,1)S(1)}, bf16[288,128]{1,0:T(8,128)(2,1)S(1)}, u32[]{:S(2)}, u32[]{:S(2)}) collective-permute-start(bf16[288,128]{1,0:T(8,128)(2,1)S(1)} %get-tuple-element.30), channel_id=1, source_target_pairs={{0,4},{1,9},{2,6},{3,11},{4,0},{5,13},{6,2},{7,15},{8,12},{9,1},{1... | collective-permute-start | bytes 221192 | tf_op jit(solution)/shard_map/ppermute | solution.py:243
  11.3 11.5 %collective-permute-start.7 = (bf16[288,128]{1,0:T(8,128)(2,1)S(1)}, bf16[288,128]{1,0:T(8,128)(2,1)S(1)}, u32[]{:S(2)}, u32[]{:S(2)}) collective-permute-start(bf16[288,128]{1,0:T(8,128)(2,1)S(1)} %get-tuple-element.34), channel_id=1, source_target_pairs={{0,12},{1,11},{2,14},{3,9},{4,8},{5,15},{6,10},{7,13},{8,4},{9,3},... | collective-permute-start | bytes 221192 | tf_op jit(solution)/shard_map/ppermute | solution.py:243
  16.2 6.6 %collective-permute-start.8 = (bf16[288,128]{1,0:T(8,128)(2,1)S(1)}, bf16[288,128]{1,0:T(8,128)(2,1)S(1)}, u32[]{:S(2)}, u32[]{:S(2)}) collective-permute-start(bf16[288,128]{1,0:T(8,128)(2,1)S(1)} %get-tuple-element.35), channel_id=1, source_target_pairs={{0,6},{1,13},{2,4},{3,15},{4,2},{5,9},{6,0},{7,11},{8,14},{9,5},{1... | collective-permute-start | bytes 221192 | tf_op jit(solution)/shard_map/ppermute | solution.py:243
  16.2 5.2 %copy-start.3 = (s32[2,4]{1,0:T(2,128)S(1)}, s32[2,4]{1,0:T(2,128)}, u32[]{:S(2)}) copy-start(s32[2,4]{1,0:T(2,128)} %lengths_ref.3) | copy-start | bytes 100
  16.2 5.2 %copy-start.4 = (s32[4]{0:T(128)S(1)}, s32[4]{0:T(128)}, u32[]{:S(2)}) copy-start(s32[4]{0:T(128)} %counts_ref.3) | copy-start | bytes 52
  16.2 7.5 %collective-permute-start.9 = (bf16[288,128]{1,0:T(8,128)(2,1)S(1)}, bf16[288,128]{1,0:T(8,128)(2,1)S(1)}, u32[]{:S(2)}, u32[]{:S(2)}) collective-permute-start(bf16[288,128]{1,0:T(8,128)(2,1)S(1)} %get-tuple-element.36), channel_id=1, source_target_pairs={{0,14},{1,15},{2,12},{3,13},{4,10},{5,11},{6,8},{7,9},{8,6},{9,7},... | collective-permute-start | bytes 221192 | tf_op jit(solution)/shard_map/ppermute | solution.py:243
  27.2 15.2 %copy-start.2 = (bf16[1024,64]{0,1:T(8,128)(2,1)S(1)}, bf16[1024,64]{0,1:T(8,128)(2,1)}, u32[]{:S(2)}) copy-start(bf16[1024,64]{0,1:T(8,128)(2,1)} %param.23) | copy-start | bytes 393220
  27.2 15.2 %all-to-all-start = ((bf16[16,48,128]{2,1,0:T(8,128)(2,1)}), bf16[16,48,128]{2,1,0:T(8,128)(2,1)S(1)}, u32[]{:S(2)}, u32[]{:S(2)}) async-start(bf16[16,48,128]{2,1,0:T(8,128)(2,1)} %bitcast.3), calls=%async_computation | async-start | bytes 393216 | tf_op jit(solution)/shard_map/all_to_all | solution.py:290
  33.4 1.4 %collective-permute-start = (bf16[48,1024]{1,0:T(8,128)(2,1)S(1)}, bf16[48,1024]{1,0:T(8,128)(2,1)S(1)}, u32[]{:S(2)}, u32[]{:S(2)}) collective-permute-start(bf16[48,1024]{1,0:T(8,128)(2,1)S(1)} %get-tuple-element.22), channel_id=1, source_target_pairs={{0,1},{1,0},{2,3},{3,2},{4,5},{5,4},{6,7},{7,6},{8,9},{9,8},{10,11... | collective-permute-start | bytes 294920 | tf_op jit(solution)/shard_map/ppermute | solution.py:246
where the time goes:
time: 43.7 us; the launch traced here: 43.4 us
  starting transfers between devices  22.2 us (51%)
  waiting for transfers between devices  13 us (30%)
  Pallas kernels  7.51 us (17%)
  between operations  0.73 us (2%)
    ppermute x7, starting transfers between devices, local(): lax.ppermute(blocks[index], 'seq', chip_pairs(devices, index))  15 us
    all_to_all x1, waiting for transfers between devices, local(): lax.all_to_all(attended.reshape(devices, tok // 2, HEAD_CHANNELS), 'seq',...  7.53 us
    all_to_all x1, starting transfers between devices, local(): lax.all_to_all(attended.reshape(devices, tok // 2, HEAD_CHANNELS), 'seq',...  6.24 us
    ppermute x7, waiting for transfers between devices, local(): lax.ppermute(blocks[index], 'seq', chip_pairs(devices, index))  5.07 us
    pallas_call x1, Pallas kernels, local(): pl.pallas_call(functools.partial(attend_kernel, chips), out_shape=jax.Sha...  3.55 us
    pallas_call x1, Pallas kernels, local(): pl.pallas_call(functools.partial(pack_kernel, chips), out_shape=[block_sh...  1.5 us
    pallas_call x1, Pallas kernels, local(): pl.pallas_call(functools.partial(early_kernel, chips), out_shape=[jax.Sha...  1.45 us
    pallas_call x1, Pallas kernels, local(): pl.pallas_call(functools.partial(head_kernel, chips), out_shape=jax.Shape...  1.02 us
  transfers between devices with their start and end apart: 11, of which 6 were waited for; matrix products, arithmetic and copies ran while one was open for 0% of the time, Pallas kernels for 7%

commit v1 on v0

--- a/solution.py
+++ b/solution.py
@@ -27,15 +27,16 @@
 
 
 def chip_pairs(devices, index):
-    return [(d, d ^ (2 * hop(index, devices // 2, d % 2))) for d in range(devices)]
+    return [(d, d ^ (2 * hop(index, devices // 2))) for d in range(devices)]
 
 
 def core_pairs(devices):
     return [(source, source ^ 1) for source in range(devices)]
 
 
-def hop(index, chips, core):
-    return (1 - core) * (index // 2 + (index % 2) * (chips // 2)) + core * (index)
+def hop(index, chips):
+    near = index // 2
+    return near + (index % 2) * (chips - 1 - 2 * near)
 
 
 def my_chip():
@@ -53,21 +54,16 @@
 
 
 def pack_kernel(chips, *refs):
-    sources, small, residual = refs[:3], refs[3:6], refs[6]
-    blocks, kept, (own, other, sems) = refs[7 : 7 + chips], refs[7 + chips : 10 + chips], refs[10 + chips :]
+    sources, blocks, sems = refs[:3], refs[3 : 3 + chips], refs[3 + chips]
     tok = sources[0].shape[0]
-    chip, core = my_chip(), my_core()
+    chip = my_chip()
     copies = []
     for index in range(chips):
-        head = chip ^ hop(index, chips, core)
+        head = chip ^ hop(index, chips)
         cols = pl.ds(pl.multiple_of(head * HEAD_CHANNELS, HEAD_CHANNELS), HEAD_CHANNELS)
         for part, source in enumerate(sources):
             target = blocks[index].at[pl.ds(part * tok, tok)]
             copies.append(pltpu.make_async_copy(source.at[:, cols], target, sems.at[len(copies)]))
-    half = tok // 2
-    halves = [residual.at[pl.ds(pl.multiple_of(c * half, 16), half)] for c in (core, 1 - core)]
-    for source, target in zip(list(small) + halves, list(kept) + [own, other]):
-        copies.append(pltpu.make_async_copy(source, target, sems.at[len(copies)]))
     for copy in copies:
         copy.start()
     for copy in copies:
@@ -102,21 +98,35 @@
 
 
 def video_of(place, ends):
+    place = jnp.int32(place) if isinstance(place, int) else place
     return sum((place >= e).astype(jnp.int32) for e in ends[:-1])
 
 
-def prompt(queries, keys, values, length):
-    scores = jnp.dot(queries, keys, preferred_element_type=jnp.float32)
-    place = lax.broadcasted_iota(jnp.int32, (1, keys.shape[1]), 1)
-    return dot_last(softmax(jnp.where(place < length, scores, -1e30)), values)
+def prompts(picked, raw, shares):
+    tok, text = picked[0][0].shape[0], raw.shape[1]
+    place = lax.broadcasted_iota(jnp.int32, (1, text), 1)
+    for i, (queries, keys, _, _) in enumerate(picked):
+        raw[pl.ds(i * tok, tok), :] = jnp.dot(queries, keys, preferred_element_type=jnp.float32)
+    for i, (_, _, _, length) in enumerate(picked):
+        for frame in range(tok // TPF):
+            at = pl.ds(i * tok + frame * TPF, TPF)
+            shares[at, :] = softmax(jnp.where(place < length, raw[at, :], -1e30))
+    return [dot_last(shares[pl.ds(i * tok, tok), :], p[2]) for i, p in enumerate(picked)]
 
 
 def early_kernel(chips, counts_ref, lengths_ref, tk_own, tv_own, tk_other, tv_other, *rest):
-    blocks = rest[:-4]
-    cross, tk, tv, qs = rest[-4:]
-    early, tok = cross.shape[:2]
+    early, tok = rest[-11].shape[:2]
+    small, residual, blocks = rest[:3], rest[3], rest[4 : 4 + early]
+    cross, tk, tv, *kept, own, other, raw, shares, sems = rest[4 + early :]
     videos, half = tk_own.shape[1:3]
     chip, core = my_chip(), my_core()
+    sides = [residual.at[pl.ds(pl.multiple_of(c * (tok // 2), 16), tok // 2)] for c in (core, 1 - core)]
+    copies = [
+        pltpu.make_async_copy(source, target, sems.at[i])
+        for i, (source, target) in enumerate(zip((*small, *sides), (*kept, own, other)))
+    ]
+    for copy in copies:
+        copy.start()
     ends = video_ends(counts_ref)
     own_rows = pl.ds(pl.multiple_of(core * half, half), half)
     other_rows = pl.ds(pl.multiple_of((1 - core) * half, half), half)
@@ -125,55 +135,59 @@
         tk[video, other_rows, :] = tk_other[core, video]
         tv[video, own_rows, :] = tv_own[core, video]
         tv[video, other_rows, :] = tv_other[core, video]
+    picked = []
     for index in range(early):
-        qs[index] = blocks[index][pl.ds(0, tok), :]
-
-    def one(index, carry):
-        video = video_of((chip ^ hop(index, chips, core)) * tok, ends)
-        cross[index] = prompt(qs[index], tk[video], tv[video], lengths_ref[core, video])
-        return carry
-
-    repeat(early, one)
+        video = video_of((chip ^ hop(index, chips)) * tok, ends)
+        queries = blocks[index][pl.ds(0, tok), :]
+        picked.append((queries, tk[video], tv[video], lengths_ref[core, video]))
+    for index, out in enumerate(prompts(picked, raw, shares)):
+        cross[index] = out
+    for copy in copies:
+        copy.wait()
 
 
 def attend_kernel(chips, counts_ref, lengths_ref, tk, tv, early_ref, *rest):
     blocks, out_ref = rest[:chips], rest[chips]
-    qs, ks, vs, cross, raw, weights = rest[chips + 1 :]
+    qs, ks, vs, cross, raw, weights, prompt_raw, shares = rest[chips + 1 :]
     tok = cross.shape[1]
     total = chips * tok
     strip = raw.shape[0]
     chip, core = my_chip(), my_core()
     ends = video_ends(counts_ref)
     for index in range(chips):
-        h = chip ^ hop(index, chips, core)
+        h = chip ^ hop(index, chips)
         at = rows(h * tok, tok)
         for part, target in enumerate((qs, ks, vs)):
             target[at, :] = blocks[index][pl.ds(part * tok, tok), :]
 
-    def prompt_of(h, video):
+    def pick(h, video):
         queries = qs[rows(h * tok, tok), :]
-        return prompt(queries, tk[video], tv[video], lengths_ref[core, video])
-
-    for index in range(chips):
-        h = chip ^ hop(index, chips, core)
-        if index < early_ref.shape[0]:
-            cross[h] = early_ref[index]
-        else:
-            cross[h] = prompt_of(h, video_of(h * tok, ends))
-    for video in range(1, len(ends)):
-        h = ends[video - 1] // tok
-        row_video = video_of(h * tok + lax.broadcasted_iota(jnp.int32, (tok, 1), 0), ends)
-        cross[h] = jnp.where(row_video == video, prompt_of(h, video), cross[h])
+        return queries, tk[video], tv[video], lengths_ref[core, video]
+
+    early = early_ref.shape[0]
+    late = [chip ^ hop(index, chips) for index in range(early, chips)]
+    begun = [ends[video - 1] // tok for video in range(1, len(ends))]
+    picked = [pick(h, video_of(h * tok, ends)) for h in late]
+    picked += [pick(h, video + 1) for video, h in enumerate(begun)]
+    found = prompts(picked, prompt_raw, shares)
+    for index in range(early):
+        cross[chip ^ hop(index, chips)] = early_ref[index]
+    for h, out in zip(late, found):
+        cross[h] = out
+    for video, (h, out) in enumerate(zip(begun, found[len(late) :])):
+        for frame in range(tok // TPF):
+            at = pl.ds(frame * TPF, TPF)
+            here = video_of(h * tok + frame * TPF, ends) == video + 1
+            cross[h, at, :] = jnp.where(here, out[frame * TPF : (frame + 1) * TPF], cross[h, at, :])
 
     key_video = video_of(lax.broadcasted_iota(jnp.int32, (1, total), 1), ends)
 
     def one_strip(index, carry):
         base = index * strip
         raw[...] = dot_last(qs[rows(base, strip), :], ks[...])
-        for b in range(strip // tok):
-            at = pl.ds(b * tok, tok)
-            place = base + b * tok + lax.broadcasted_iota(jnp.int32, (tok, 1), 0)
-            allowed = video_of(place, ends) == key_video
+        for frame in range(strip // TPF):
+            at = pl.ds(frame * TPF, TPF)
+            allowed = key_video == video_of(base + frame * TPF, ends)
             weights[at, :] = softmax(jnp.where(allowed, raw[at, :], -1e30))
         out = jnp.dot(weights[...], vs[...], preferred_element_type=jnp.float32)
         for b in range(strip // tok):
@@ -230,36 +244,39 @@
     vectors = (mod_gain, mod_shift, head_bias)
     packed = pl.pallas_call(
         functools.partial(pack_kernel, chips),
-        out_shape=[block_shape] * chips + [jax.ShapeDtypeStruct(v.shape, v.dtype) for v in vectors]
-        + [jax.ShapeDtypeStruct((tok // 2, width), bf16)] * 2,
-        in_specs=[HBM] * 7,
-        out_specs=[VMEM] * (chips + 5),
-        scratch_shapes=[pltpu.SemaphoreType.DMA((3 * chips + 5,))],
+        out_shape=[block_shape] * chips,
+        in_specs=[HBM] * 3,
+        out_specs=[VMEM] * chips,
+        scratch_shapes=[pltpu.SemaphoreType.DMA((3 * chips,))],
         compiler_params=params(8),
         name="pack",
-    )(*(pltpu.with_memory_space_constraint(x, pltpu.HBM) for x in (queries, self_keys, self_values) + vectors + (residual_in,)))
-    blocks, vectors, (x_own, x_other) = list(packed[:chips]), packed[chips:-2], packed[-2:]
+    )(*(pltpu.with_memory_space_constraint(x, pltpu.HBM) for x in (queries, self_keys, self_values)))
+    blocks = list(packed)
     for index in range(1, chips):
         blocks[index] = lax.ppermute(blocks[index], "seq", chip_pairs(devices, index))
     other_keys = lax.ppermute(text_keys, "seq", core_pairs(devices))
     other_values = lax.ppermute(text_values, "seq", core_pairs(devices))
-    x_other = lax.ppermute(x_other, "seq", core_pairs(devices))
-
     videos, half, text = text_keys.shape[1:]
     tokens = pltpu.VMEM((total, HEAD_CHANNELS), bf16)
     strip = math.gcd(chips, STRIP) * tok
     early = max(chips - LATE, 1)
-    prompts = jax.ShapeDtypeStruct((videos, 2 * half, text), bf16)
-    cross, keys, values = pl.pallas_call(
+    joined = jax.ShapeDtypeStruct((videos, 2 * half, text), bf16)
+    cross, keys, values, *vectors, x_own, x_other = pl.pallas_call(
         functools.partial(early_kernel, chips),
         out_shape=[
             jax.ShapeDtypeStruct((early, tok, HEAD_CHANNELS), f32),
-            prompts,
-            prompts,
+            joined,
+            joined,
+        ]
+        + [jax.ShapeDtypeStruct(v.shape, v.dtype) for v in vectors]
+        + [jax.ShapeDtypeStruct((tok // 2, width), bf16)] * 2,
+        in_specs=[SMEM] * 2 + [VMEM] * 4 + [HBM] * 4 + [VMEM] * early,
+        out_specs=[VMEM] * 8,
+        scratch_shapes=[
+            pltpu.VMEM((early * tok, text), f32),
+            pltpu.VMEM((early * tok, text), bf16),
+            pltpu.SemaphoreType.DMA((5,)),
         ],
-        in_specs=[SMEM] * 2 + [VMEM] * (4 + early),
-        out_specs=[VMEM] * 3,
-        scratch_shapes=[pltpu.VMEM((early, tok, HEAD_CHANNELS), bf16)],
         cost_estimate=pl.CostEstimate(
             flops=4 * early * tok * text * HEAD_CHANNELS,
             bytes_accessed=4 * total * HEAD_CHANNELS,
@@ -267,7 +284,17 @@
         ),
         compiler_params=params(12),
         name="early",
-    )(frame_counts, text_lengths, text_keys, text_values, other_keys, other_values, *blocks[:early])
+    )(
+        frame_counts,
+        text_lengths,
+        text_keys,
+        text_values,
+        other_keys,
+        other_values,
+        *(pltpu.with_memory_space_constraint(x, pltpu.HBM) for x in (*vectors, residual_in)),
+        *blocks[:early],
+    )
+    x_other = lax.ppermute(x_other, "seq", core_pairs(devices))
     attended = pl.pallas_call(
         functools.partial(attend_kernel, chips),
         out_shape=jax.ShapeDtypeStruct((chips, tok, HEAD_CHANNELS), bf16),
@@ -278,6 +305,8 @@
             pltpu.VMEM((chips, tok, HEAD_CHANNELS), f32),
             pltpu.VMEM((strip, total), f32),
             pltpu.VMEM((strip, total), bf16),
+            pltpu.VMEM(((chips - early + videos - 1) * tok, text), f32),
+            pltpu.VMEM(((chips - early + videos - 1) * tok, text), bf16),
         ],
         cost_estimate=pl.CostEstimate(
             flops=4 * total * total * HEAD_CHANNELS,

time: 43.7 us -> 41.9 us (0.959)
  waiting for transfers between devices: 13 us -> 11.7 us
  starting transfers between devices: 22.2 us -> 21.7 us
    ppermute x7, waiting for transfers between devices: 5.07 us -> 3.75 us  [local(): lax.ppermute(blocks[index], 'seq', chip_pairs(devices, index))]
    ppermute x7, starting transfers between devices: 15 us -> 14 us  [local(): lax.ppermute(blocks[index], 'seq', chip_pairs(devices, index))]
    pallas_call x1, Pallas kernels: 1.45 us -> 2 us  [local(): pl.pallas_call(functools.partial(early_kernel, chips), out_shape=[jax.Sha...]
    all_to_all x1, starting transfers between devices: 6.24 us -> 6.77 us  [local(): lax.all_to_all(attended.reshape(devices, tok // 2, HEAD_CHANNELS), 'seq',...]
    pallas_call x1, Pallas kernels: 3.55 us -> 3.11 us  [local(): pl.pallas_call(functools.partial(attend_kernel, chips), out_shape=jax.Sha...]
  transfers between devices with their start and end apart: 11 -> 11, of which waited for: 6 -> 5; matrix products, arithmetic and copies ran while one was open for 0% -> 0% of each run, Pallas kernels for 7% -> 8%
where the time goes in v1:
time: 41.9 us; the launch traced here: 41.5 us
  starting transfers between devices  21.7 us (52%)
  waiting for transfers between devices  11.7 us (28%)
  Pallas kernels  7.39 us (18%)
  between operations  0.74 us (2%)
    ppermute x7, starting transfers between devices, local(): lax.ppermute(blocks[index], 'seq', chip_pairs(devices, index))  14 us
    all_to_all x1, waiting for transfers between devices, local(): lax.all_to_all(attended.reshape(devices, tok // 2, HEAD_CHANNELS), 'seq',...  7.53 us
    all_to_all x1, starting transfers between devices, local(): lax.all_to_all(attended.reshape(devices, tok // 2, HEAD_CHANNELS), 'seq',...  6.77 us
    ppermute x7, waiting for transfers between devices, local(): lax.ppermute(blocks[index], 'seq', chip_pairs(devices, index))  3.75 us
    pallas_call x1, Pallas kernels, local(): pl.pallas_call(functools.partial(attend_kernel, chips), out_shape=jax.Sha...  3.11 us
    pallas_call x1, Pallas kernels, local(): pl.pallas_call(functools.partial(early_kernel, chips), out_shape=[jax.Sha...  2 us
    pallas_call x1, Pallas kernels, local(): pl.pallas_call(functools.partial(pack_kernel, chips), out_shape=[block_sh...  1.27 us
    pallas_call x1, Pallas kernels, local(): pl.pallas_call(functools.partial(head_kernel, chips), out_shape=jax.Shape...  1.02 us
  transfers between devices with their start and end apart: 11, of which 5 were waited for; matrix products, arithmetic and copies ran while one was open for 0% of the time, Pallas kernels for 8%

profile of v1, /device:TPU:0, one launch (start us, length us, event | category | flops | bytes accessed | tf_op | source)
XLA Modules:
  0.0 41.5 jit_solution(12593648637814556412)
XLA Ops:
  0.0 0.5 %collective-permute-start = (bf16[2,4,64,256]{3,2,1,0:T(8,128)(2,1)}, bf16[2,4,64,256]{3,2,1,0:T(8,128)(2,1)S(1)}, u32[]{:S(2)}, u32[]{:S(2)}) collective-permute-start(bf16[2,4,64,256]{3,2,1,0:T(8,128)(2,1)} %bitcast.4), channel_id=1, source_target_pairs={{0,1},{1,0},{2,3},{3,2},{4,5},{5,4},{6,7},{7,6},{8,9},{9,8},{10,11... | collective-permute-start | bytes 786440 | tf_op jit(solution)/shard_map/ppermute | solution.py:257
  0.5 0.0 copy-start
  0.5 0.0 copy-start.1
  0.5 0.1 collective-permute-start.1
  0.6 1.3 %pack.1 = (bf16[288,128]{1,0:T(8,128)(2,1)S(1)}, bf16[288,128]{1,0:T(8,128)(2,1)S(1)}, bf16[288,128]{1,0:T(8,128)(2,1)S(1)}, bf16[288,128]{1,0:T(8,128)(2,1)S(1)...) custom-call(bf16[96,1024]{1,0:T(8,128)(2,1)} %refs_0_.1, ...), custom_call_target="tpu_custom_call" | custom-call | tf_op jit(solution)/shard_map/pack/pallas_call | solution.py:245
  1.8 6.0 %collective-permute-start.2 = (bf16[288,128]{1,0:T(8,128)(2,1)S(1)}, bf16[288,128]{1,0:T(8,128)(2,1)S(1)}, u32[]{:S(2)}, u32[]{:S(2)}) collective-permute-start(bf16[288,128]{1,0:T(8,128)(2,1)S(1)} %get-tuple-element.22), channel_id=1, source_target_pairs={{0,14},{1,15},{2,12},{3,13},{4,10},{5,11},{6,8},{7,9},{8,6},{9,7},... | collective-permute-start | bytes 221192 | tf_op jit(solution)/shard_map/ppermute | solution.py:256
  7.9 0.5 %collective-permute-start.3 = (bf16[288,128]{1,0:T(8,128)(2,1)S(1)}, bf16[288,128]{1,0:T(8,128)(2,1)S(1)}, u32[]{:S(2)}, u32[]{:S(2)}) collective-permute-start(bf16[288,128]{1,0:T(8,128)(2,1)S(1)} %get-tuple-element.23), channel_id=1, source_target_pairs={{0,2},{1,3},{2,0},{3,1},{4,6},{5,7},{6,4},{7,5},{8,10},{9,11},{10,... | collective-permute-start | bytes 221192 | tf_op jit(solution)/shard_map/ppermute | solution.py:256
  8.4 0.1 collective-permute-start.4
  8.5 2.1 %collective-permute-done.2.rest_5_.rest_1_ = bf16[288,128]{1,0:T(8,128)(2,1)S(1)} collective-permute-done((bf16[288,128]{1,0:T(8,128)(2,1)S(1)}, bf16[288,128]{1,0:T(8,128)(2,1)S(1)}, u32[]{:S(2)}, u32[]{:S(2)}) %collective-permute-start.2) | collective-permute-done | bytes 73760 | tf_op jit(solution)/shard_map/ppermute | solution.py:256
  10.6 2.0 %collective-permute-start.5 = (bf16[288,128]{1,0:T(8,128)(2,1)S(1)}, bf16[288,128]{1,0:T(8,128)(2,1)S(1)}, u32[]{:S(2)}, u32[]{:S(2)}) collective-permute-start(bf16[288,128]{1,0:T(8,128)(2,1)S(1)} %get-tuple-element.25), channel_id=1, source_target_pairs={{0,4},{1,5},{2,6},{3,7},{4,0},{5,1},{6,2},{7,3},{8,12},{9,13},{10,... | collective-permute-start | bytes 221192 | tf_op jit(solution)/shard_map/ppermute | solution.py:256
  12.6 0.0 collective-permute-done.3.rest_6_.rest_2_
  12.6 3.7 %collective-permute-start.7 = (bf16[288,128]{1,0:T(8,128)(2,1)S(1)}, bf16[288,128]{1,0:T(8,128)(2,1)S(1)}, u32[]{:S(2)}, u32[]{:S(2)}) collective-permute-start(bf16[288,128]{1,0:T(8,128)(2,1)S(1)} %get-tuple-element.34), channel_id=1, source_target_pairs={{0,10},{1,11},{2,8},{3,9},{4,14},{5,15},{6,12},{7,13},{8,2},{9,3},... | collective-permute-start | bytes 221192 | tf_op jit(solution)/shard_map/ppermute | solution.py:256
  16.3 0.0 collective-permute-done.4.rest_7_.rest_3_
  16.3 0.0 collective-permute-start.8
  16.3 0.0 collective-permute-done.5.rest_8_.rest_4_
  16.3 0.0 copy-start.3
  16.3 0.0 copy-start.4
  16.3 1.6 %collective-permute-start.9 = (bf16[288,128]{1,0:T(8,128)(2,1)S(1)}, bf16[288,128]{1,0:T(8,128)(2,1)S(1)}, u32[]{:S(2)}, u32[]{:S(2)}) collective-permute-start(bf16[288,128]{1,0:T(8,128)(2,1)S(1)} %get-tuple-element.36), channel_id=1, source_target_pairs={{0,8},{1,9},{2,10},{3,11},{4,12},{5,13},{6,14},{7,15},{8,0},{9,1},... | collective-permute-start | bytes 221192 | tf_op jit(solution)/shard_map/ppermute | solution.py:256
  17.9 0.0 collective-permute-done.tk_other
  17.9 0.0 collective-permute-done.1.tv_other
  17.9 0.0 copy-done
  17.9 0.0 copy-done.1
  18.0 0.0 copy-done.3
  18.0 0.0 copy-done.4
  18.0 2.0 %early.1 = (f32[5,96,128]{2,1,0:T(8,128)S(1)}, bf16[4,128,256]{2,1,0:T(8,128)(2,1)S(1)}, bf16[4,128,256]{2,1,0:T(8,128)(2,1)S(1)}, f32[1024]{0:T(1024)S(1)}, f32...) custom-call(s32[4]{0:T(128)S(1)} %copy-done.4, ...), custom_call_target="tpu_custom_call" | custom-call | flops 62914560 | bytes 393216 | tf_op jit(solution)/shard_map/early/pallas_call | solution.py:264
  20.0 0.0 collective-permute-done.7.rest_5_
  20.0 1.6 %collective-permute-done.8.rest_6_ = bf16[288,128]{1,0:T(8,128)(2,1)S(1)} collective-permute-done((bf16[288,128]{1,0:T(8,128)(2,1)S(1)}, bf16[288,128]{1,0:T(8,128)(2,1)S(1)}, u32[]{:S(2)}, u32[]{:S(2)}) %collective-permute-start.8) | collective-permute-done | bytes 73760 | tf_op jit(solution)/shard_map/ppermute | solution.py:256
  21.6 0.1 collective-permute-done.9.rest_7_
  21.7 3.1 %attend.1 = bf16[8,96,128]{2,1,0:T(8,128)(2,1)} custom-call(s32[4]{0:T(128)S(1)} %copy-done.4, s32[2,4]{1,0:T(2,128)S(1)} %copy-done.3, bf16[4,128,256]{2,1,0:T(8,128)(2,1)S(1)} %get-tuple-element.31.tk, bf16[4,128,256]{2,1,0:T(8,128)(2,1)S(1)} %get-tuple-element.32.tv, f32[5,96,128]{2,1,0:T(8,128)S(1)} %get-tuple-element.33.early_ref, ...), custom_call_target="tpu_custom_call" | custom-call | flops 301989888 | bytes 786432 | tf_op jit(solution)/shard_map/attend/pallas_call | solution.py:298
  24.8 0.0 copy-start.2
  24.8 6.8 %all-to-all-start = ((bf16[16,48,128]{2,1,0:T(8,128)(2,1)}), bf16[16,48,128]{2,1,0:T(8,128)(2,1)S(1)}, u32[]{:S(2)}, u32[]{:S(2)}) async-start(bf16[16,48,128]{2,1,0:T(8,128)(2,1)} %bitcast.3), calls=%async_computation | async-start | bytes 393216 | tf_op jit(solution)/shard_map/all_to_all | solution.py:319
  31.6 0.4 collective-permute-start.6
  32.6 0.4 collective-permute-done.6.x_other
  33.0 7.5 %all-to-all-done.blocks = bf16[16,48,128]{2,1,0:T(8,128)(2,1)S(1)} async-done(((bf16[16,48,128]{2,1,0:T(8,128)(2,1)}), bf16[16,48,128]{2,1,0:T(8,128)(2,1)S(1)}, u32[]{:S(2)}, u32[]{:S(2)}) %all-to-all-start) | async-done | bytes 196640 | tf_op jit(solution)/shard_map/all_to_all | solution.py:319
  40.5 0.0 copy-done.2
  40.5 1.0 %head.1 = f32[48,64]{1,0:T(8,128)} custom-call(f32[1]{0:T(128)S(6)} %copy.14.scale_ref, bf16[48,1024]{1,0:T(8,128)(2,1)S(1)} %get-tuple-element.26.x_ref, bf16[48,1024]{1,0:T(8,128)(2,1)S(1)} %collective-permute-done.6.x_other, f32[1024]{0:T(1024)S(1)} %get-tuple-element.28.gain_ref, f32[1024]{0:T(1024)S(1)} %get-tuple-element.29.shift_ref, ...), custom_call_target="tpu_custom_call" | custom-call | tf_op jit(solution)/shard_map/head/pallas_call | solution.py:323
Async XLA Ops:
  0.0 17.9 %collective-permute-start = (bf16[2,4,64,256]{3,2,1,0:T(8,128)(2,1)}, bf16[2,4,64,256]{3,2,1,0:T(8,128)(2,1)S(1)}, u32[]{:S(2)}, u32[]{:S(2)}) collective-permute-start(bf16[2,4,64,256]{3,2,1,0:T(8,128)(2,1)} %bitcast.4), channel_id=1, source_target_pairs={{0,1},{1,0},{2,3},{3,2},{4,5},{5,4},{6,7},{7,6},{8,9},{9,8},{10,11... | collective-permute-start | bytes 786440 | tf_op jit(solution)/shard_map/ppermute | solution.py:257
  0.5 17.4 %copy-start = (bf16[2,4,256,64]{2,3,1,0:T(8,128)(2,1)S(1)}, bf16[2,4,256,64]{2,3,1,0:T(8,128)(2,1)}, u32[]{:S(2)}) copy-start(bf16[2,4,256,64]{2,3,1,0:T(8,128)(2,1)} %param.17) | copy-start | bytes 786436
  0.5 17.4 %copy-start.1 = (bf16[2,4,256,64]{2,3,1,0:T(8,128)(2,1)S(1)}, bf16[2,4,256,64]{2,3,1,0:T(8,128)(2,1)}, u32[]{:S(2)}) copy-start(bf16[2,4,256,64]{2,3,1,0:T(8,128)(2,1)} %param.18) | copy-start | bytes 786436
  0.5 17.4 %collective-permute-start.1 = (bf16[2,4,64,256]{3,2,1,0:T(8,128)(2,1)}, bf16[2,4,64,256]{3,2,1,0:T(8,128)(2,1)S(1)}, u32[]{:S(2)}, u32[]{:S(2)}) collective-permute-start(bf16[2,4,64,256]{3,2,1,0:T(8,128)(2,1)} %bitcast.6), channel_id=1, source_target_pairs={{0,1},{1,0},{2,3},{3,2},{4,5},{5,4},{6,7},{7,6},{8,9},{9,8},{10,11... | collective-permute-start | bytes 786440 | tf_op jit(solution)/shard_map/ppermute | solution.py:258
  1.8 8.7 %collective-permute-start.2 = (bf16[288,128]{1,0:T(8,128)(2,1)S(1)}, bf16[288,128]{1,0:T(8,128)(2,1)S(1)}, u32[]{:S(2)}, u32[]{:S(2)}) collective-permute-start(bf16[288,128]{1,0:T(8,128)(2,1)S(1)} %get-tuple-element.22), channel_id=1, source_target_pairs={{0,14},{1,15},{2,12},{3,13},{4,10},{5,11},{6,8},{7,9},{8,6},{9,7},... | collective-permute-start | bytes 221192 | tf_op jit(solution)/shard_map/ppermute | solution.py:256
  7.9 4.7 %collective-permute-start.3 = (bf16[288,128]{1,0:T(8,128)(2,1)S(1)}, bf16[288,128]{1,0:T(8,128)(2,1)S(1)}, u32[]{:S(2)}, u32[]{:S(2)}) collective-permute-start(bf16[288,128]{1,0:T(8,128)(2,1)S(1)} %get-tuple-element.23), channel_id=1, source_target_pairs={{0,2},{1,3},{2,0},{3,1},{4,6},{5,7},{6,4},{7,5},{8,10},{9,11},{10,... | collective-permute-start | bytes 221192 | tf_op jit(solution)/shard_map/ppermute | solution.py:256
  8.4 7.9 %collective-permute-start.4 = (bf16[288,128]{1,0:T(8,128)(2,1)S(1)}, bf16[288,128]{1,0:T(8,128)(2,1)S(1)}, u32[]{:S(2)}, u32[]{:S(2)}) collective-permute-start(bf16[288,128]{1,0:T(8,128)(2,1)S(1)} %get-tuple-element.24), channel_id=1, source_target_pairs={{0,12},{1,13},{2,14},{3,15},{4,8},{5,9},{6,10},{7,11},{8,4},{9,5},... | collective-permute-start | bytes 221192 | tf_op jit(solution)/shard_map/ppermute | solution.py:256
  10.6 5.8 %collective-permute-start.5 = (bf16[288,128]{1,0:T(8,128)(2,1)S(1)}, bf16[288,128]{1,0:T(8,128)(2,1)S(1)}, u32[]{:S(2)}, u32[]{:S(2)}) collective-permute-start(bf16[288,128]{1,0:T(8,128)(2,1)S(1)} %get-tuple-element.25), channel_id=1, source_target_pairs={{0,4},{1,5},{2,6},{3,7},{4,0},{5,1},{6,2},{7,3},{8,12},{9,13},{10,... | collective-permute-start | bytes 221192 | tf_op jit(solution)/shard_map/ppermute | solution.py:256
  12.6 7.4 %collective-permute-start.7 = (bf16[288,128]{1,0:T(8,128)(2,1)S(1)}, bf16[288,128]{1,0:T(8,128)(2,1)S(1)}, u32[]{:S(2)}, u32[]{:S(2)}) collective-permute-start(bf16[288,128]{1,0:T(8,128)(2,1)S(1)} %get-tuple-element.34), channel_id=1, source_target_pairs={{0,10},{1,11},{2,8},{3,9},{4,14},{5,15},{6,12},{7,13},{8,2},{9,3},... | collective-permute-start | bytes 221192 | tf_op jit(solution)/shard_map/ppermute | solution.py:256
  16.3 5.3 %collective-permute-start.8 = (bf16[288,128]{1,0:T(8,128)(2,1)S(1)}, bf16[288,128]{1,0:T(8,128)(2,1)S(1)}, u32[]{:S(2)}, u32[]{:S(2)}) collective-permute-start(bf16[288,128]{1,0:T(8,128)(2,1)S(1)} %get-tuple-element.35), channel_id=1, source_target_pairs={{0,6},{1,7},{2,4},{3,5},{4,2},{5,3},{6,0},{7,1},{8,14},{9,15},{10,... | collective-permute-start | bytes 221192 | tf_op jit(solution)/shard_map/ppermute | solution.py:256
  16.3 1.6 %copy-start.3 = (s32[2,4]{1,0:T(2,128)S(1)}, s32[2,4]{1,0:T(2,128)}, u32[]{:S(2)}) copy-start(s32[2,4]{1,0:T(2,128)} %lengths_ref.3) | copy-start | bytes 100
  16.3 1.6 %copy-start.4 = (s32[4]{0:T(128)S(1)}, s32[4]{0:T(128)}, u32[]{:S(2)}) copy-start(s32[4]{0:T(128)} %counts_ref.3) | copy-start | bytes 52
  16.3 5.3 %collective-permute-start.9 = (bf16[288,128]{1,0:T(8,128)(2,1)S(1)}, bf16[288,128]{1,0:T(8,128)(2,1)S(1)}, u32[]{:S(2)}, u32[]{:S(2)}) collective-permute-start(bf16[288,128]{1,0:T(8,128)(2,1)S(1)} %get-tuple-element.36), channel_id=1, source_target_pairs={{0,8},{1,9},{2,10},{3,11},{4,12},{5,13},{6,14},{7,15},{8,0},{9,1},... | collective-permute-start | bytes 221192 | tf_op jit(solution)/shard_map/ppermute | solution.py:256
  24.8 15.7 %copy-start.2 = (bf16[1024,64]{0,1:T(8,128)(2,1)S(1)}, bf16[1024,64]{0,1:T(8,128)(2,1)}, u32[]{:S(2)}) copy-start(bf16[1024,64]{0,1:T(8,128)(2,1)} %param.23) | copy-start | bytes 393220
  24.8 15.7 %all-to-all-start = ((bf16[16,48,128]{2,1,0:T(8,128)(2,1)}), bf16[16,48,128]{2,1,0:T(8,128)(2,1)S(1)}, u32[]{:S(2)}, u32[]{:S(2)}) async-start(bf16[16,48,128]{2,1,0:T(8,128)(2,1)} %bitcast.3), calls=%async_computation | async-start | bytes 393216 | tf_op jit(solution)/shard_map/all_to_all | solution.py:319
  31.6 1.4 %collective-permute-start.6 = (bf16[48,1024]{1,0:T(8,128)(2,1)S(1)}, bf16[48,1024]{1,0:T(8,128)(2,1)S(1)}, u32[]{:S(2)}, u32[]{:S(2)}) collective-permute-start(bf16[48,1024]{1,0:T(8,128)(2,1)S(1)} %get-tuple-element.27), channel_id=1, source_target_pairs={{0,1},{1,0},{2,3},{3,2},{4,5},{5,4},{6,7},{7,6},{8,9},{9,8},{10,11... | collective-permute-start | bytes 294920 | tf_op jit(solution)/shard_map/ppermute | solution.py:297

commit v2 on v1

--- a/solution.py
+++ b/solution.py
@@ -15,6 +15,7 @@
 UNROLL_CHIPS = 8
 STRIP = 8
 LATE = 3
+LEAD = 4
 
 
 def params(mib):
@@ -37,6 +38,14 @@
 def hop(index, chips):
     near = index // 2
     return near + (index % 2) * (chips - 1 - 2 * near)
+
+
+def lead(chips):
+    return chips * LEAD // 8
+
+
+def place_of(chip, chips):
+    return (chip + chips - lead(chips)) % chips
 
 
 def my_chip():
@@ -192,7 +201,7 @@
         out = jnp.dot(weights[...], vs[...], preferred_element_type=jnp.float32)
         for b in range(strip // tok):
             h = index * (strip // tok) + b
-            out_ref[h] = (out[b * tok : (b + 1) * tok] + cross[h]).astype(jnp.bfloat16)
+            out_ref[place_of(h, chips)] = (out[b * tok : (b + 1) * tok] + cross[h]).astype(jnp.bfloat16)
         return carry
 
     repeat(total // strip, one_strip)
@@ -204,7 +213,7 @@
     gain, shift = (ref[...].reshape(1, width) for ref in (gain_ref, shift_ref))
 
     def velocity(x, branch):
-        attention = jnp.concatenate([blocks[2 * h + branch] for h in range(chips)], axis=-1)
+        attention = jnp.concatenate([blocks[2 * place_of(h, chips) + branch] for h in range(chips)], axis=-1)
         hidden = x.astype(jnp.float32) + attention.astype(jnp.float32)
         mean = jnp.sum(hidden, axis=-1, keepdims=True) * (1.0 / width)
         centred = hidden - mean
@@ -317,7 +326,12 @@
         name="attend",
     )(frame_counts, text_lengths, keys, values, cross, *blocks)
     returned = lax.all_to_all(
-        attended.reshape(devices, tok // 2, HEAD_CHANNELS), "seq", split_axis=0, concat_axis=0, tiled=True
+        attended.reshape(devices, tok // 2, HEAD_CHANNELS),
+        "seq",
+        split_axis=0,
+        concat_axis=0,
+        axis_index_groups=[[(d + 2 * lead(chips)) % devices for d in range(devices)]],
+        tiled=True,
     )
 
     return pl.pallas_call(

time: 41.9 us -> 40 us (0.955)
  waiting for transfers between devices: 11.7 us -> 9.68 us
    all_to_all x1, waiting for transfers between devices: 7.53 us -> 5.39 us  [local(): lax.all_to_all(attended.reshape(devices, tok // 2, HEAD_CHANNELS), 'seq',...]
    all_to_all x1, starting transfers between devices: 6.77 us -> 7.25 us  [local(): lax.all_to_all(attended.reshape(devices, tok // 2, HEAD_CHANNELS), 'seq',...]
where the time goes in v2:
time: 40 us; the launch traced here: 39.7 us
  starting transfers between devices  21.9 us (55%)
  waiting for transfers between devices  9.68 us (24%)
  Pallas kernels  7.39 us (18%)
  between operations  0.73 us (2%)
    ppermute x7, starting transfers between devices, local(): lax.ppermute(blocks[index], 'seq', chip_pairs(devices, index))  14 us
    all_to_all x1, starting transfers between devices, local(): lax.all_to_all(attended.reshape(devices, tok // 2, HEAD_CHANNELS), 'seq',...  7.25 us
    all_to_all x1, waiting for transfers between devices, local(): lax.all_to_all(attended.reshape(devices, tok // 2, HEAD_CHANNELS), 'seq',...  5.39 us
    ppermute x7, waiting for transfers between devices, local(): lax.ppermute(blocks[index], 'seq', chip_pairs(devices, index))  3.75 us
    pallas_call x1, Pallas kernels, local(): pl.pallas_call(functools.partial(attend_kernel, chips), out_shape=jax.Sha...  3.11 us
    pallas_call x1, Pallas kernels, local(): pl.pallas_call(functools.partial(early_kernel, chips), out_shape=[jax.Sha...  2 us
    pallas_call x1, Pallas kernels, local(): pl.pallas_call(functools.partial(pack_kernel, chips), out_shape=[block_sh...  1.27 us
    pallas_call x1, Pallas kernels, local(): pl.pallas_call(functools.partial(head_kernel, chips), out_shape=jax.Shape...  1.02 us
  transfers between devices with their start and end apart: 11, of which 5 were waited for; matrix products, arithmetic and copies ran while one was open for 0% of the time, Pallas kernels for 8%

profile of v2, /device:TPU:0, one launch (start us, length us, event | category | flops | bytes accessed | tf_op | source)
XLA Modules:
  0.0 39.7 jit_solution(18135603788628770857)
XLA Ops:
  0.0 0.5 %collective-permute-start = (bf16[2,4,64,256]{3,2,1,0:T(8,128)(2,1)}, bf16[2,4,64,256]{3,2,1,0:T(8,128)(2,1)S(1)}, u32[]{:S(2)}, u32[]{:S(2)}) collective-permute-start(bf16[2,4,64,256]{3,2,1,0:T(8,128)(2,1)} %bitcast.4), channel_id=1, source_target_pairs={{0,1},{1,0},{2,3},{3,2},{4,5},{5,4},{6,7},{7,6},{8,9},{9,8},{10,11... | collective-permute-start | bytes 786440 | tf_op jit(solution)/shard_map/ppermute | solution.py:266
  0.5 0.0 copy-start
  0.5 0.0 copy-start.1
  0.5 0.1 collective-permute-start.1
  0.6 1.3 %pack.1 = (bf16[288,128]{1,0:T(8,128)(2,1)S(1)}, bf16[288,128]{1,0:T(8,128)(2,1)S(1)}, bf16[288,128]{1,0:T(8,128)(2,1)S(1)}, bf16[288,128]{1,0:T(8,128)(2,1)S(1)...) custom-call(bf16[96,1024]{1,0:T(8,128)(2,1)} %refs_0_.1, ...), custom_call_target="tpu_custom_call" | custom-call | tf_op jit(solution)/shard_map/pack/pallas_call | solution.py:254
  1.8 6.0 %collective-permute-start.2 = (bf16[288,128]{1,0:T(8,128)(2,1)S(1)}, bf16[288,128]{1,0:T(8,128)(2,1)S(1)}, u32[]{:S(2)}, u32[]{:S(2)}) collective-permute-start(bf16[288,128]{1,0:T(8,128)(2,1)S(1)} %get-tuple-element.22), channel_id=1, source_target_pairs={{0,14},{1,15},{2,12},{3,13},{4,10},{5,11},{6,8},{7,9},{8,6},{9,7},... | collective-permute-start | bytes 221192 | tf_op jit(solution)/shard_map/ppermute | solution.py:265
  7.9 0.5 %collective-permute-start.3 = (bf16[288,128]{1,0:T(8,128)(2,1)S(1)}, bf16[288,128]{1,0:T(8,128)(2,1)S(1)}, u32[]{:S(2)}, u32[]{:S(2)}) collective-permute-start(bf16[288,128]{1,0:T(8,128)(2,1)S(1)} %get-tuple-element.23), channel_id=1, source_target_pairs={{0,2},{1,3},{2,0},{3,1},{4,6},{5,7},{6,4},{7,5},{8,10},{9,11},{10,... | collective-permute-start | bytes 221192 | tf_op jit(solution)/shard_map/ppermute | solution.py:265
  8.4 0.1 collective-permute-start.4
  8.5 2.1 %collective-permute-done.2.rest_5_.rest_1_ = bf16[288,128]{1,0:T(8,128)(2,1)S(1)} collective-permute-done((bf16[288,128]{1,0:T(8,128)(2,1)S(1)}, bf16[288,128]{1,0:T(8,128)(2,1)S(1)}, u32[]{:S(2)}, u32[]{:S(2)}) %collective-permute-start.2) | collective-permute-done | bytes 73760 | tf_op jit(solution)/shard_map/ppermute | solution.py:265
  10.6 2.0 %collective-permute-start.5 = (bf16[288,128]{1,0:T(8,128)(2,1)S(1)}, bf16[288,128]{1,0:T(8,128)(2,1)S(1)}, u32[]{:S(2)}, u32[]{:S(2)}) collective-permute-start(bf16[288,128]{1,0:T(8,128)(2,1)S(1)} %get-tuple-element.25), channel_id=1, source_target_pairs={{0,4},{1,5},{2,6},{3,7},{4,0},{5,1},{6,2},{7,3},{8,12},{9,13},{10,... | collective-permute-start | bytes 221192 | tf_op jit(solution)/shard_map/ppermute | solution.py:265
  12.6 0.0 collective-permute-done.3.rest_6_.rest_2_
  12.6 3.7 %collective-permute-start.7 = (bf16[288,128]{1,0:T(8,128)(2,1)S(1)}, bf16[288,128]{1,0:T(8,128)(2,1)S(1)}, u32[]{:S(2)}, u32[]{:S(2)}) collective-permute-start(bf16[288,128]{1,0:T(8,128)(2,1)S(1)} %get-tuple-element.34), channel_id=1, source_target_pairs={{0,10},{1,11},{2,8},{3,9},{4,14},{5,15},{6,12},{7,13},{8,2},{9,3},... | collective-permute-start | bytes 221192 | tf_op jit(solution)/shard_map/ppermute | solution.py:265
  16.3 0.0 collective-permute-done.4.rest_7_.rest_3_
  16.3 0.0 collective-permute-start.8
  16.3 0.0 collective-permute-done.5.rest_8_.rest_4_
  16.3 0.0 copy-start.3
  16.3 0.0 copy-start.4
  16.3 1.6 %collective-permute-start.9 = (bf16[288,128]{1,0:T(8,128)(2,1)S(1)}, bf16[288,128]{1,0:T(8,128)(2,1)S(1)}, u32[]{:S(2)}, u32[]{:S(2)}) collective-permute-start(bf16[288,128]{1,0:T(8,128)(2,1)S(1)} %get-tuple-element.36), channel_id=1, source_target_pairs={{0,8},{1,9},{2,10},{3,11},{4,12},{5,13},{6,14},{7,15},{8,0},{9,1},... | collective-permute-start | bytes 221192 | tf_op jit(solution)/shard_map/ppermute | solution.py:265
  17.9 0.0 collective-permute-done.tk_other
  17.9 0.0 collective-permute-done.1.tv_other
  17.9 0.0 copy-done
  17.9 0.0 copy-done.1
  18.0 0.0 copy-done.3
  18.0 0.0 copy-done.4
  18.0 2.0 %early.1 = (f32[5,96,128]{2,1,0:T(8,128)S(1)}, bf16[4,128,256]{2,1,0:T(8,128)(2,1)S(1)}, bf16[4,128,256]{2,1,0:T(8,128)(2,1)S(1)}, f32[1024]{0:T(1024)S(1)}, f32...) custom-call(s32[4]{0:T(128)S(1)} %copy-done.4, ...), custom_call_target="tpu_custom_call" | custom-call | flops 62914560 | bytes 393216 | tf_op jit(solution)/shard_map/early/pallas_call | solution.py:273
  20.0 0.0 collective-permute-done.7.rest_5_
  20.0 1.6 %collective-permute-done.8.rest_6_ = bf16[288,128]{1,0:T(8,128)(2,1)S(1)} collective-permute-done((bf16[288,128]{1,0:T(8,128)(2,1)S(1)}, bf16[288,128]{1,0:T(8,128)(2,1)S(1)}, u32[]{:S(2)}, u32[]{:S(2)}) %collective-permute-start.8) | collective-permute-done | bytes 73760 | tf_op jit(solution)/shard_map/ppermute | solution.py:265
  21.6 0.1 collective-permute-done.9.rest_7_
  21.7 3.1 %attend.1 = bf16[8,96,128]{2,1,0:T(8,128)(2,1)} custom-call(s32[4]{0:T(128)S(1)} %copy-done.4, s32[2,4]{1,0:T(2,128)S(1)} %copy-done.3, bf16[4,128,256]{2,1,0:T(8,128)(2,1)S(1)} %get-tuple-element.31.tk, bf16[4,128,256]{2,1,0:T(8,128)(2,1)S(1)} %get-tuple-element.32.tv, f32[5,96,128]{2,1,0:T(8,128)S(1)} %get-tuple-element.33.early_ref, ...), custom_call_target="tpu_custom_call" | custom-call | flops 301989888 | bytes 786432 | tf_op jit(solution)/shard_map/attend/pallas_call | solution.py:307
  24.8 0.0 copy-start.2
  24.8 7.2 %all-to-all-start = ((bf16[16,48,128]{2,1,0:T(8,128)(2,1)}), bf16[16,48,128]{2,1,0:T(8,128)(2,1)S(1)}, u32[]{:S(2)}, u32[]{:S(2)}) async-start(bf16[16,48,128]{2,1,0:T(8,128)(2,1)} %bitcast.3), calls=%async_computation | async-start | bytes 393216 | tf_op jit(solution)/shard_map/all_to_all | solution.py:328
  32.0 0.1 collective-permute-start.6
  32.8 0.5 %collective-permute-done.6.x_other = bf16[48,1024]{1,0:T(8,128)(2,1)S(1)} collective-permute-done((bf16[48,1024]{1,0:T(8,128)(2,1)S(1)}, bf16[48,1024]{1,0:T(8,128)(2,1)S(1)}, u32[]{:S(2)}, u32[]{:S(2)}) %collective-permute-start.6) | collective-permute-done | bytes 98336 | tf_op jit(solution)/shard_map/ppermute | solution.py:306
  33.3 5.4 %all-to-all-done.blocks = bf16[16,48,128]{2,1,0:T(8,128)(2,1)S(1)} async-done(((bf16[16,48,128]{2,1,0:T(8,128)(2,1)}), bf16[16,48,128]{2,1,0:T(8,128)(2,1)S(1)}, u32[]{:S(2)}, u32[]{:S(2)}) %all-to-all-start) | async-done | bytes 196640 | tf_op jit(solution)/shard_map/all_to_all | solution.py:328
  38.7 0.0 copy-done.2
  38.7 1.0 %head.1 = f32[48,64]{1,0:T(8,128)} custom-call(f32[1]{0:T(128)S(6)} %copy.14.scale_ref, bf16[48,1024]{1,0:T(8,128)(2,1)S(1)} %get-tuple-element.26.x_ref, bf16[48,1024]{1,0:T(8,128)(2,1)S(1)} %collective-permute-done.6.x_other, f32[1024]{0:T(1024)S(1)} %get-tuple-element.28.gain_ref, f32[1024]{0:T(1024)S(1)} %get-tuple-element.29.shift_ref, ...), custom_call_target="tpu_custom_call" | custom-call | tf_op jit(solution)/shard_map/head/pallas_call | solution.py:337
Async XLA Ops:
  0.0 17.9 %collective-permute-start = (bf16[2,4,64,256]{3,2,1,0:T(8,128)(2,1)}, bf16[2,4,64,256]{3,2,1,0:T(8,128)(2,1)S(1)}, u32[]{:S(2)}, u32[]{:S(2)}) collective-permute-start(bf16[2,4,64,256]{3,2,1,0:T(8,128)(2,1)} %bitcast.4), channel_id=1, source_target_pairs={{0,1},{1,0},{2,3},{3,2},{4,5},{5,4},{6,7},{7,6},{8,9},{9,8},{10,11... | collective-permute-start | bytes 786440 | tf_op jit(solution)/shard_map/ppermute | solution.py:266
  0.5 17.4 %copy-start = (bf16[2,4,256,64]{2,3,1,0:T(8,128)(2,1)S(1)}, bf16[2,4,256,64]{2,3,1,0:T(8,128)(2,1)}, u32[]{:S(2)}) copy-start(bf16[2,4,256,64]{2,3,1,0:T(8,128)(2,1)} %param.17) | copy-start | bytes 786436
  0.5 17.4 %copy-start.1 = (bf16[2,4,256,64]{2,3,1,0:T(8,128)(2,1)S(1)}, bf16[2,4,256,64]{2,3,1,0:T(8,128)(2,1)}, u32[]{:S(2)}) copy-start(bf16[2,4,256,64]{2,3,1,0:T(8,128)(2,1)} %param.18) | copy-start | bytes 786436
  0.5 17.4 %collective-permute-start.1 = (bf16[2,4,64,256]{3,2,1,0:T(8,128)(2,1)}, bf16[2,4,64,256]{3,2,1,0:T(8,128)(2,1)S(1)}, u32[]{:S(2)}, u32[]{:S(2)}) collective-permute-start(bf16[2,4,64,256]{3,2,1,0:T(8,128)(2,1)} %bitcast.6), channel_id=1, source_target_pairs={{0,1},{1,0},{2,3},{3,2},{4,5},{5,4},{6,7},{7,6},{8,9},{9,8},{10,11... | collective-permute-start | bytes 786440 | tf_op jit(solution)/shard_map/ppermute | solution.py:267
  1.8 8.7 %collective-permute-start.2 = (bf16[288,128]{1,0:T(8,128)(2,1)S(1)}, bf16[288,128]{1,0:T(8,128)(2,1)S(1)}, u32[]{:S(2)}, u32[]{:S(2)}) collective-permute-start(bf16[288,128]{1,0:T(8,128)(2,1)S(1)} %get-tuple-element.22), channel_id=1, source_target_pairs={{0,14},{1,15},{2,12},{3,13},{4,10},{5,11},{6,8},{7,9},{8,6},{9,7},... | collective-permute-start | bytes 221192 | tf_op jit(solution)/shard_map/ppermute | solution.py:265
  7.9 4.7 %collective-permute-start.3 = (bf16[288,128]{1,0:T(8,128)(2,1)S(1)}, bf16[288,128]{1,0:T(8,128)(2,1)S(1)}, u32[]{:S(2)}, u32[]{:S(2)}) collective-permute-start(bf16[288,128]{1,0:T(8,128)(2,1)S(1)} %get-tuple-element.23), channel_id=1, source_target_pairs={{0,2},{1,3},{2,0},{3,1},{4,6},{5,7},{6,4},{7,5},{8,10},{9,11},{10,... | collective-permute-start | bytes 221192 | tf_op jit(solution)/shard_map/ppermute | solution.py:265
  8.4 7.9 %collective-permute-start.4 = (bf16[288,128]{1,0:T(8,128)(2,1)S(1)}, bf16[288,128]{1,0:T(8,128)(2,1)S(1)}, u32[]{:S(2)}, u32[]{:S(2)}) collective-permute-start(bf16[288,128]{1,0:T(8,128)(2,1)S(1)} %get-tuple-element.24), channel_id=1, source_target_pairs={{0,12},{1,13},{2,14},{3,15},{4,8},{5,9},{6,10},{7,11},{8,4},{9,5},... | collective-permute-start | bytes 221192 | tf_op jit(solution)/shard_map/ppermute | solution.py:265
  10.6 5.8 %collective-permute-start.5 = (bf16[288,128]{1,0:T(8,128)(2,1)S(1)}, bf16[288,128]{1,0:T(8,128)(2,1)S(1)}, u32[]{:S(2)}, u32[]{:S(2)}) collective-permute-start(bf16[288,128]{1,0:T(8,128)(2,1)S(1)} %get-tuple-element.25), channel_id=1, source_target_pairs={{0,4},{1,5},{2,6},{3,7},{4,0},{5,1},{6,2},{7,3},{8,12},{9,13},{10,... | collective-permute-start | bytes 221192 | tf_op jit(solution)/shard_map/ppermute | solution.py:265
  12.6 7.4 %collective-permute-start.7 = (bf16[288,128]{1,0:T(8,128)(2,1)S(1)}, bf16[288,128]{1,0:T(8,128)(2,1)S(1)}, u32[]{:S(2)}, u32[]{:S(2)}) collective-permute-start(bf16[288,128]{1,0:T(8,128)(2,1)S(1)} %get-tuple-element.34), channel_id=1, source_target_pairs={{0,10},{1,11},{2,8},{3,9},{4,14},{5,15},{6,12},{7,13},{8,2},{9,3},... | collective-permute-start | bytes 221192 | tf_op jit(solution)/shard_map/ppermute | solution.py:265
  16.3 5.3 %collective-permute-start.8 = (bf16[288,128]{1,0:T(8,128)(2,1)S(1)}, bf16[288,128]{1,0:T(8,128)(2,1)S(1)}, u32[]{:S(2)}, u32[]{:S(2)}) collective-permute-start(bf16[288,128]{1,0:T(8,128)(2,1)S(1)} %get-tuple-element.35), channel_id=1, source_target_pairs={{0,6},{1,7},{2,4},{3,5},{4,2},{5,3},{6,0},{7,1},{8,14},{9,15},{10,... | collective-permute-start | bytes 221192 | tf_op jit(solution)/shard_map/ppermute | solution.py:265
  16.3 1.6 %copy-start.3 = (s32[2,4]{1,0:T(2,128)S(1)}, s32[2,4]{1,0:T(2,128)}, u32[]{:S(2)}) copy-start(s32[2,4]{1,0:T(2,128)} %lengths_ref.3) | copy-start | bytes 100
  16.3 1.6 %copy-start.4 = (s32[4]{0:T(128)S(1)}, s32[4]{0:T(128)}, u32[]{:S(2)}) copy-start(s32[4]{0:T(128)} %counts_ref.3) | copy-start | bytes 52
  16.3 5.3 %collective-permute-start.9 = (bf16[288,128]{1,0:T(8,128)(2,1)S(1)}, bf16[288,128]{1,0:T(8,128)(2,1)S(1)}, u32[]{:S(2)}, u32[]{:S(2)}) collective-permute-start(bf16[288,128]{1,0:T(8,128)(2,1)S(1)} %get-tuple-element.36), channel_id=1, source_target_pairs={{0,8},{1,9},{2,10},{3,11},{4,12},{5,13},{6,14},{7,15},{8,0},{9,1},... | collective-permute-start | bytes 221192 | tf_op jit(solution)/shard_map/ppermute | solution.py:265
  24.8 13.9 %copy-start.2 = (bf16[1024,64]{0,1:T(8,128)(2,1)S(1)}, bf16[1024,64]{0,1:T(8,128)(2,1)}, u32[]{:S(2)}) copy-start(bf16[1024,64]{0,1:T(8,128)(2,1)} %param.23) | copy-start | bytes 393220
  24.8 13.9 %all-to-all-start = ((bf16[16,48,128]{2,1,0:T(8,128)(2,1)}), bf16[16,48,128]{2,1,0:T(8,128)(2,1)S(1)}, u32[]{:S(2)}, u32[]{:S(2)}) async-start(bf16[16,48,128]{2,1,0:T(8,128)(2,1)} %bitcast.3), calls=%async_computation | async-start | bytes 393216 | tf_op jit(solution)/shard_map/all_to_all | solution.py:328
  32.0 1.3 %collective-permute-start.6 = (bf16[48,1024]{1,0:T(8,128)(2,1)S(1)}, bf16[48,1024]{1,0:T(8,128)(2,1)S(1)}, u32[]{:S(2)}, u32[]{:S(2)}) collective-permute-start(bf16[48,1024]{1,0:T(8,128)(2,1)S(1)} %get-tuple-element.27), channel_id=1, source_target_pairs={{0,1},{1,0},{2,3},{3,2},{4,5},{5,4},{6,7},{7,6},{8,9},{9,8},{10,11... | collective-permute-start | bytes 294920 | tf_op jit(solution)/shard_map/ppermute | solution.py:306

commit v3 on v2

--- a/solution.py
+++ b/solution.py
@@ -201,7 +201,8 @@
         out = jnp.dot(weights[...], vs[...], preferred_element_type=jnp.float32)
         for b in range(strip // tok):
             h = index * (strip // tok) + b
-            out_ref[place_of(h, chips)] = (out[b * tok : (b + 1) * tok] + cross[h]).astype(jnp.bfloat16)
+            whole = (out[b * tok : (b + 1) * tok] + cross[h]).astype(jnp.bfloat16)
+            out_ref[place_of(h, chips)] = jnp.concatenate([whole[tok // 2 :], whole[: tok // 2]])
         return carry
 
     repeat(total // strip, one_strip)
@@ -213,7 +214,7 @@
     gain, shift = (ref[...].reshape(1, width) for ref in (gain_ref, shift_ref))
 
     def velocity(x, branch):
-        attention = jnp.concatenate([blocks[2 * place_of(h, chips) + branch] for h in range(chips)], axis=-1)
+        attention = jnp.concatenate([blocks[2 * place_of(h, chips) + 1 - branch] for h in range(chips)], axis=-1)
         hidden = x.astype(jnp.float32) + attention.astype(jnp.float32)
         mean = jnp.sum(hidden, axis=-1, keepdims=True) * (1.0 / width)
         centred = hidden - mean
@@ -330,7 +331,7 @@
         "seq",
         split_axis=0,
         concat_axis=0,
-        axis_index_groups=[[(d + 2 * lead(chips)) % devices for d in range(devices)]],
+        axis_index_groups=[[((d + 2 * lead(chips)) % devices) ^ 1 for d in range(devices)]],
         tiled=True,
     )
 

time: 40 us -> 39.8 us (level)
  no operation moved by 1% of the time
where the time goes in v3:
time: 39.8 us; the launch traced here: 39.5 us
  starting transfers between devices  21.6 us (54%)
  waiting for transfers between devices  9.68 us (24%)
  Pallas kernels  7.4 us (19%)
  between operations  0.73 us (2%)
    ppermute x7, starting transfers between devices, local(): lax.ppermute(blocks[index], 'seq', chip_pairs(devices, index))  14 us
    all_to_all x1, starting transfers between devices, local(): lax.all_to_all(attended.reshape(devices, tok // 2, HEAD_CHANNELS), 'seq',...  6.97 us
    all_to_all x1, waiting for transfers between devices, local(): lax.all_to_all(attended.reshape(devices, tok // 2, HEAD_CHANNELS), 'seq',...  5.39 us
    ppermute x7, waiting for transfers between devices, local(): lax.ppermute(blocks[index], 'seq', chip_pairs(devices, index))  3.75 us
    pallas_call x1, Pallas kernels, local(): pl.pallas_call(functools.partial(attend_kernel, chips), out_shape=jax.Sha...  3.11 us
    pallas_call x1, Pallas kernels, local(): pl.pallas_call(functools.partial(early_kernel, chips), out_shape=[jax.Sha...  2 us
    pallas_call x1, Pallas kernels, local(): pl.pallas_call(functools.partial(pack_kernel, chips), out_shape=[block_sh...  1.27 us
    pallas_call x1, Pallas kernels, local(): pl.pallas_call(functools.partial(head_kernel, chips), out_shape=jax.Shape...  1.02 us
  transfers between devices with their start and end apart: 11, of which 5 were waited for; matrix products, arithmetic and copies ran while one was open for 0% of the time, Pallas kernels for 8%

profile of v3, /device:TPU:0, one launch (start us, length us, event | category | flops | bytes accessed | tf_op | source)
XLA Modules:
  0.0 39.5 jit_solution(5141790872415593583)
XLA Ops:
  0.0 0.5 %collective-permute-start = (bf16[2,4,64,256]{3,2,1,0:T(8,128)(2,1)}, bf16[2,4,64,256]{3,2,1,0:T(8,128)(2,1)S(1)}, u32[]{:S(2)}, u32[]{:S(2)}) collective-permute-start(bf16[2,4,64,256]{3,2,1,0:T(8,128)(2,1)} %bitcast.4), channel_id=1, source_target_pairs={{0,1},{1,0},{2,3},{3,2},{4,5},{5,4},{6,7},{7,6},{8,9},{9,8},{10,11... | collective-permute-start | bytes 786440 | tf_op jit(solution)/shard_map/ppermute | solution.py:267
  0.5 0.0 copy-start
  0.5 0.0 copy-start.1
  0.5 0.1 collective-permute-start.1
  0.6 1.3 %pack.1 = (bf16[288,128]{1,0:T(8,128)(2,1)S(1)}, bf16[288,128]{1,0:T(8,128)(2,1)S(1)}, bf16[288,128]{1,0:T(8,128)(2,1)S(1)}, bf16[288,128]{1,0:T(8,128)(2,1)S(1)...) custom-call(bf16[96,1024]{1,0:T(8,128)(2,1)} %refs_0_.1, ...), custom_call_target="tpu_custom_call" | custom-call | tf_op jit(solution)/shard_map/pack/pallas_call | solution.py:255
  1.8 6.0 %collective-permute-start.2 = (bf16[288,128]{1,0:T(8,128)(2,1)S(1)}, bf16[288,128]{1,0:T(8,128)(2,1)S(1)}, u32[]{:S(2)}, u32[]{:S(2)}) collective-permute-start(bf16[288,128]{1,0:T(8,128)(2,1)S(1)} %get-tuple-element.22), channel_id=1, source_target_pairs={{0,14},{1,15},{2,12},{3,13},{4,10},{5,11},{6,8},{7,9},{8,6},{9,7},... | collective-permute-start | bytes 221192 | tf_op jit(solution)/shard_map/ppermute | solution.py:266
  7.9 0.5 %collective-permute-start.3 = (bf16[288,128]{1,0:T(8,128)(2,1)S(1)}, bf16[288,128]{1,0:T(8,128)(2,1)S(1)}, u32[]{:S(2)}, u32[]{:S(2)}) collective-permute-start(bf16[288,128]{1,0:T(8,128)(2,1)S(1)} %get-tuple-element.23), channel_id=1, source_target_pairs={{0,2},{1,3},{2,0},{3,1},{4,6},{5,7},{6,4},{7,5},{8,10},{9,11},{10,... | collective-permute-start | bytes 221192 | tf_op jit(solution)/shard_map/ppermute | solution.py:266
  8.4 0.1 collective-permute-start.4
  8.5 2.1 %collective-permute-done.2.rest_5_.rest_1_ = bf16[288,128]{1,0:T(8,128)(2,1)S(1)} collective-permute-done((bf16[288,128]{1,0:T(8,128)(2,1)S(1)}, bf16[288,128]{1,0:T(8,128)(2,1)S(1)}, u32[]{:S(2)}, u32[]{:S(2)}) %collective-permute-start.2) | collective-permute-done | bytes 73760 | tf_op jit(solution)/shard_map/ppermute | solution.py:266
  10.6 2.0 %collective-permute-start.5 = (bf16[288,128]{1,0:T(8,128)(2,1)S(1)}, bf16[288,128]{1,0:T(8,128)(2,1)S(1)}, u32[]{:S(2)}, u32[]{:S(2)}) collective-permute-start(bf16[288,128]{1,0:T(8,128)(2,1)S(1)} %get-tuple-element.25), channel_id=1, source_target_pairs={{0,4},{1,5},{2,6},{3,7},{4,0},{5,1},{6,2},{7,3},{8,12},{9,13},{10,... | collective-permute-start | bytes 221192 | tf_op jit(solution)/shard_map/ppermute | solution.py:266
  12.6 0.0 collective-permute-done.3.rest_6_.rest_2_
  12.6 3.7 %collective-permute-start.7 = (bf16[288,128]{1,0:T(8,128)(2,1)S(1)}, bf16[288,128]{1,0:T(8,128)(2,1)S(1)}, u32[]{:S(2)}, u32[]{:S(2)}) collective-permute-start(bf16[288,128]{1,0:T(8,128)(2,1)S(1)} %get-tuple-element.34), channel_id=1, source_target_pairs={{0,10},{1,11},{2,8},{3,9},{4,14},{5,15},{6,12},{7,13},{8,2},{9,3},... | collective-permute-start | bytes 221192 | tf_op jit(solution)/shard_map/ppermute | solution.py:266
  16.3 0.0 collective-permute-done.4.rest_7_.rest_3_
  16.3 0.0 collective-permute-start.8
  16.3 0.0 collective-permute-done.5.rest_8_.rest_4_
  16.3 0.0 copy-start.3
  16.3 0.0 copy-start.4
  16.3 1.6 %collective-permute-start.9 = (bf16[288,128]{1,0:T(8,128)(2,1)S(1)}, bf16[288,128]{1,0:T(8,128)(2,1)S(1)}, u32[]{:S(2)}, u32[]{:S(2)}) collective-permute-start(bf16[288,128]{1,0:T(8,128)(2,1)S(1)} %get-tuple-element.36), channel_id=1, source_target_pairs={{0,8},{1,9},{2,10},{3,11},{4,12},{5,13},{6,14},{7,15},{8,0},{9,1},... | collective-permute-start | bytes 221192 | tf_op jit(solution)/shard_map/ppermute | solution.py:266
  17.9 0.0 collective-permute-done.tk_other
  17.9 0.0 collective-permute-done.1.tv_other
  17.9 0.0 copy-done
  17.9 0.0 copy-done.1
  18.0 0.0 copy-done.3
  18.0 0.0 copy-done.4
  18.0 2.0 %early.1 = (f32[5,96,128]{2,1,0:T(8,128)S(1)}, bf16[4,128,256]{2,1,0:T(8,128)(2,1)S(1)}, bf16[4,128,256]{2,1,0:T(8,128)(2,1)S(1)}, f32[1024]{0:T(1024)S(1)}, f32...) custom-call(s32[4]{0:T(128)S(1)} %copy-done.4, ...), custom_call_target="tpu_custom_call" | custom-call | flops 62914560 | bytes 393216 | tf_op jit(solution)/shard_map/early/pallas_call | solution.py:274
  20.0 0.0 collective-permute-done.7.rest_5_
  20.0 1.6 %collective-permute-done.8.rest_6_ = bf16[288,128]{1,0:T(8,128)(2,1)S(1)} collective-permute-done((bf16[288,128]{1,0:T(8,128)(2,1)S(1)}, bf16[288,128]{1,0:T(8,128)(2,1)S(1)}, u32[]{:S(2)}, u32[]{:S(2)}) %collective-permute-start.8) | collective-permute-done | bytes 73760 | tf_op jit(solution)/shard_map/ppermute | solution.py:266
  21.6 0.1 collective-permute-done.9.rest_7_
  21.7 3.1 %attend.1 = bf16[8,96,128]{2,1,0:T(8,128)(2,1)} custom-call(s32[4]{0:T(128)S(1)} %copy-done.4, s32[2,4]{1,0:T(2,128)S(1)} %copy-done.3, bf16[4,128,256]{2,1,0:T(8,128)(2,1)S(1)} %get-tuple-element.31.tk, bf16[4,128,256]{2,1,0:T(8,128)(2,1)S(1)} %get-tuple-element.32.tv, f32[5,96,128]{2,1,0:T(8,128)S(1)} %get-tuple-element.33.early_ref, ...), custom_call_target="tpu_custom_call" | custom-call | flops 301989888 | bytes 786432 | tf_op jit(solution)/shard_map/attend/pallas_call | solution.py:308
  24.8 0.0 copy-start.2
  24.8 7.0 %all-to-all-start = ((bf16[16,48,128]{2,1,0:T(8,128)(2,1)}), bf16[16,48,128]{2,1,0:T(8,128)(2,1)S(1)}, u32[]{:S(2)}, u32[]{:S(2)}) async-start(bf16[16,48,128]{2,1,0:T(8,128)(2,1)} %bitcast.3), calls=%async_computation | async-start | bytes 393216 | tf_op jit(solution)/shard_map/all_to_all | solution.py:329
  31.7 0.1 collective-permute-start.6
  32.5 0.5 %collective-permute-done.6.x_other = bf16[48,1024]{1,0:T(8,128)(2,1)S(1)} collective-permute-done((bf16[48,1024]{1,0:T(8,128)(2,1)S(1)}, bf16[48,1024]{1,0:T(8,128)(2,1)S(1)}, u32[]{:S(2)}, u32[]{:S(2)}) %collective-permute-start.6) | collective-permute-done | bytes 98336 | tf_op jit(solution)/shard_map/ppermute | solution.py:307
  33.1 5.4 %all-to-all-done.blocks = bf16[16,48,128]{2,1,0:T(8,128)(2,1)S(1)} async-done(((bf16[16,48,128]{2,1,0:T(8,128)(2,1)}), bf16[16,48,128]{2,1,0:T(8,128)(2,1)S(1)}, u32[]{:S(2)}, u32[]{:S(2)}) %all-to-all-start) | async-done | bytes 196640 | tf_op jit(solution)/shard_map/all_to_all | solution.py:329
  38.4 0.0 copy-done.2
  38.4 1.0 %head.1 = f32[48,64]{1,0:T(8,128)} custom-call(f32[1]{0:T(128)S(6)} %copy.14.scale_ref, bf16[48,1024]{1,0:T(8,128)(2,1)S(1)} %get-tuple-element.26.x_ref, bf16[48,1024]{1,0:T(8,128)(2,1)S(1)} %collective-permute-done.6.x_other, f32[1024]{0:T(1024)S(1)} %get-tuple-element.28.gain_ref, f32[1024]{0:T(1024)S(1)} %get-tuple-element.29.shift_ref, ...), custom_call_target="tpu_custom_call" | custom-call | tf_op jit(solution)/shard_map/head/pallas_call | solution.py:338
Async XLA Ops:
  0.0 17.9 %collective-permute-start = (bf16[2,4,64,256]{3,2,1,0:T(8,128)(2,1)}, bf16[2,4,64,256]{3,2,1,0:T(8,128)(2,1)S(1)}, u32[]{:S(2)}, u32[]{:S(2)}) collective-permute-start(bf16[2,4,64,256]{3,2,1,0:T(8,128)(2,1)} %bitcast.4), channel_id=1, source_target_pairs={{0,1},{1,0},{2,3},{3,2},{4,5},{5,4},{6,7},{7,6},{8,9},{9,8},{10,11... | collective-permute-start | bytes 786440 | tf_op jit(solution)/shard_map/ppermute | solution.py:267
  0.5 17.4 %copy-start = (bf16[2,4,256,64]{2,3,1,0:T(8,128)(2,1)S(1)}, bf16[2,4,256,64]{2,3,1,0:T(8,128)(2,1)}, u32[]{:S(2)}) copy-start(bf16[2,4,256,64]{2,3,1,0:T(8,128)(2,1)} %param.17) | copy-start | bytes 786436
  0.5 17.4 %copy-start.1 = (bf16[2,4,256,64]{2,3,1,0:T(8,128)(2,1)S(1)}, bf16[2,4,256,64]{2,3,1,0:T(8,128)(2,1)}, u32[]{:S(2)}) copy-start(bf16[2,4,256,64]{2,3,1,0:T(8,128)(2,1)} %param.18) | copy-start | bytes 786436
  0.5 17.4 %collective-permute-start.1 = (bf16[2,4,64,256]{3,2,1,0:T(8,128)(2,1)}, bf16[2,4,64,256]{3,2,1,0:T(8,128)(2,1)S(1)}, u32[]{:S(2)}, u32[]{:S(2)}) collective-permute-start(bf16[2,4,64,256]{3,2,1,0:T(8,128)(2,1)} %bitcast.6), channel_id=1, source_target_pairs={{0,1},{1,0},{2,3},{3,2},{4,5},{5,4},{6,7},{7,6},{8,9},{9,8},{10,11... | collective-permute-start | bytes 786440 | tf_op jit(solution)/shard_map/ppermute | solution.py:268
  1.8 8.7 %collective-permute-start.2 = (bf16[288,128]{1,0:T(8,128)(2,1)S(1)}, bf16[288,128]{1,0:T(8,128)(2,1)S(1)}, u32[]{:S(2)}, u32[]{:S(2)}) collective-permute-start(bf16[288,128]{1,0:T(8,128)(2,1)S(1)} %get-tuple-element.22), channel_id=1, source_target_pairs={{0,14},{1,15},{2,12},{3,13},{4,10},{5,11},{6,8},{7,9},{8,6},{9,7},... | collective-permute-start | bytes 221192 | tf_op jit(solution)/shard_map/ppermute | solution.py:266
  7.9 4.7 %collective-permute-start.3 = (bf16[288,128]{1,0:T(8,128)(2,1)S(1)}, bf16[288,128]{1,0:T(8,128)(2,1)S(1)}, u32[]{:S(2)}, u32[]{:S(2)}) collective-permute-start(bf16[288,128]{1,0:T(8,128)(2,1)S(1)} %get-tuple-element.23), channel_id=1, source_target_pairs={{0,2},{1,3},{2,0},{3,1},{4,6},{5,7},{6,4},{7,5},{8,10},{9,11},{10,... | collective-permute-start | bytes 221192 | tf_op jit(solution)/shard_map/ppermute | solution.py:266
  8.4 7.9 %collective-permute-start.4 = (bf16[288,128]{1,0:T(8,128)(2,1)S(1)}, bf16[288,128]{1,0:T(8,128)(2,1)S(1)}, u32[]{:S(2)}, u32[]{:S(2)}) collective-permute-start(bf16[288,128]{1,0:T(8,128)(2,1)S(1)} %get-tuple-element.24), channel_id=1, source_target_pairs={{0,12},{1,13},{2,14},{3,15},{4,8},{5,9},{6,10},{7,11},{8,4},{9,5},... | collective-permute-start | bytes 221192 | tf_op jit(solution)/shard_map/ppermute | solution.py:266
  10.6 5.8 %collective-permute-start.5 = (bf16[288,128]{1,0:T(8,128)(2,1)S(1)}, bf16[288,128]{1,0:T(8,128)(2,1)S(1)}, u32[]{:S(2)}, u32[]{:S(2)}) collective-permute-start(bf16[288,128]{1,0:T(8,128)(2,1)S(1)} %get-tuple-element.25), channel_id=1, source_target_pairs={{0,4},{1,5},{2,6},{3,7},{4,0},{5,1},{6,2},{7,3},{8,12},{9,13},{10,... | collective-permute-start | bytes 221192 | tf_op jit(solution)/shard_map/ppermute | solution.py:266
  12.6 7.4 %collective-permute-start.7 = (bf16[288,128]{1,0:T(8,128)(2,1)S(1)}, bf16[288,128]{1,0:T(8,128)(2,1)S(1)}, u32[]{:S(2)}, u32[]{:S(2)}) collective-permute-start(bf16[288,128]{1,0:T(8,128)(2,1)S(1)} %get-tuple-element.34), channel_id=1, source_target_pairs={{0,10},{1,11},{2,8},{3,9},{4,14},{5,15},{6,12},{7,13},{8,2},{9,3},... | collective-permute-start | bytes 221192 | tf_op jit(solution)/shard_map/ppermute | solution.py:266
  16.3 5.3 %collective-permute-start.8 = (bf16[288,128]{1,0:T(8,128)(2,1)S(1)}, bf16[288,128]{1,0:T(8,128)(2,1)S(1)}, u32[]{:S(2)}, u32[]{:S(2)}) collective-permute-start(bf16[288,128]{1,0:T(8,128)(2,1)S(1)} %get-tuple-element.35), channel_id=1, source_target_pairs={{0,6},{1,7},{2,4},{3,5},{4,2},{5,3},{6,0},{7,1},{8,14},{9,15},{10,... | collective-permute-start | bytes 221192 | tf_op jit(solution)/shard_map/ppermute | solution.py:266
  16.3 1.6 %copy-start.3 = (s32[2,4]{1,0:T(2,128)S(1)}, s32[2,4]{1,0:T(2,128)}, u32[]{:S(2)}) copy-start(s32[2,4]{1,0:T(2,128)} %lengths_ref.3) | copy-start | bytes 100
  16.3 1.6 %copy-start.4 = (s32[4]{0:T(128)S(1)}, s32[4]{0:T(128)}, u32[]{:S(2)}) copy-start(s32[4]{0:T(128)} %counts_ref.3) | copy-start | bytes 52
  16.3 5.3 %collective-permute-start.9 = (bf16[288,128]{1,0:T(8,128)(2,1)S(1)}, bf16[288,128]{1,0:T(8,128)(2,1)S(1)}, u32[]{:S(2)}, u32[]{:S(2)}) collective-permute-start(bf16[288,128]{1,0:T(8,128)(2,1)S(1)} %get-tuple-element.36), channel_id=1, source_target_pairs={{0,8},{1,9},{2,10},{3,11},{4,12},{5,13},{6,14},{7,15},{8,0},{9,1},... | collective-permute-start | bytes 221192 | tf_op jit(solution)/shard_map/ppermute | solution.py:266
  24.8 13.7 %copy-start.2 = (bf16[1024,64]{0,1:T(8,128)(2,1)S(1)}, bf16[1024,64]{0,1:T(8,128)(2,1)}, u32[]{:S(2)}) copy-start(bf16[1024,64]{0,1:T(8,128)(2,1)} %param.23) | copy-start | bytes 393220
  24.8 13.7 %all-to-all-start = ((bf16[16,48,128]{2,1,0:T(8,128)(2,1)}), bf16[16,48,128]{2,1,0:T(8,128)(2,1)S(1)}, u32[]{:S(2)}, u32[]{:S(2)}) async-start(bf16[16,48,128]{2,1,0:T(8,128)(2,1)} %bitcast.3), calls=%async_computation | async-start | bytes 393216 | tf_op jit(solution)/shard_map/all_to_all | solution.py:329
  31.7 1.3 %collective-permute-start.6 = (bf16[48,1024]{1,0:T(8,128)(2,1)S(1)}, bf16[48,1024]{1,0:T(8,128)(2,1)S(1)}, u32[]{:S(2)}, u32[]{:S(2)}) collective-permute-start(bf16[48,1024]{1,0:T(8,128)(2,1)S(1)} %get-tuple-element.27), channel_id=1, source_target_pairs={{0,1},{1,0},{2,3},{3,2},{4,5},{5,4},{6,7},{7,6},{8,9},{9,8},{10,11... | collective-permute-start | bytes 294920 | tf_op jit(solution)/shard_map/ppermute | solution.py:307
